TPU v7x, 32 devices: a whole 2x2x4 slice. The times are simulated.
32 devices in a mesh: rep: 8 (over z, y), shard: 4 (over x, core).
Axes of the slice: x: 2, y: 2, z: 4, core: 2. Of those that a mesh axis runs over, the one named last changes fastest.
Arguments:
- prompt: bfloat16 [8, 1024, 768], P('rep', 'shard'), may hold values from -6 to 6
- conts: bfloat16 [8, 4, 512, 768], P('rep', 'shard'), may hold values from -6 to 6
- prompt_cot: bfloat16 [8, 1024, 768], P('rep', 'shard'), may hold values from -6 to 6
- cont_cot: bfloat16 [8, 4, 512, 768], P('rep', 'shard'), may hold values from -6 to 6
- labels: int32 [8, 4], P('rep', 'shard'), may hold values from 0 to 13
- w_qkv: float32 [768, 2304], P('shard'), may hold values from -0.21875 to 0.21875
- w_out: float32 [768, 768], P('shard'), may hold values from -3.5 to 3.5
- w_in: float32 [768, 3072], P('shard'), may hold values from -0.21875 to 0.21875
- w_ffo: float32 [3072, 768], P('shard'), may hold values from -0.109375 to 0.109375
- layer_biases: float32 [6, 768], replicated, may hold values from -3 to 3
- norm_gains: float32 [2, 768], replicated, may hold values from 0.25 to 1.75
- bias_in: float32 [3072], replicated, may hold values from -3 to 3
- w_student: float32 [768, 128], replicated, may hold values from -0.21875 to 0.21875
- student_vectors: float32 [3, 128], replicated, may hold values from -4 to 4
- w_pool: float32 [128, 128], replicated, may hold values from -0.5 to 0.5
- w_class: float32 [128, 14], replicated, may hold values from -1 to 1
- bias_class: float32 [14], replicated, may hold values from -3 to 3
Outputs:
- prompt_out: bfloat16 [8, 1024, 768], P('rep', 'shard')
- cont_out: bfloat16 [8, 4, 512, 768], P('rep', 'shard')
- logits: float32 [8, 4, 14], P('rep', 'shard')
- prompt_grad: float32 [8, 1024, 768], P('rep', 'shard')
- cont_grad: float32 [8, 4, 512, 768], P('rep', 'shard')
- grad_qkv: float32 [768, 2304], P('shard')
- grad_out: float32 [768, 768], P('shard')
- grad_in: float32 [768, 3072], P('shard')
- grad_ffo: float32 [3072, 768], P('shard')
- grad_biases: float32 [6, 768], replicated
- grad_gains: float32 [2, 768], replicated
- grad_bias_in: float32 [3072], replicated
- grad_student: float32 [768, 128], replicated
- grad_student_vectors: float32 [3, 128], replicated
- grad_pool: float32 [128, 128], replicated
- grad_class: float32 [128, 14], replicated
- grad_bias_class: float32 [14], replicated
All inputs are finite; a program needn't handle non-finite values.
Results may differ from a plain program's by a relative error of at most 0.02.
Values may be sent and summed in bfloat16 or wider, within the bound.
A program may use at most 192 MiB of HBM per device.

v0:
```python
import jax
import jax.numpy as jnp
from jax import lax
from jax.sharding import PartitionSpec as P

D = 768
HEADS = 12
DH = 64
STU = 128
SHEADS = 2


HIGHEST = lax.Precision.HIGHEST
NEG_BIG = -1e30


def dot_plain(left, right):
    return jnp.dot(left, right, preferred_element_type=jnp.float32)


def dot_first(left, right):
    return lax.dot_general(
        left, right, (((0,), (0,)), ((), ())), preferred_element_type=jnp.float32
    )


def dot_second(left, right):
    return lax.dot_general(
        left, right, (((1,), (1,)), ((), ())), preferred_element_type=jnp.float32
    )


def column_slice(matrix, head_index):
    return lax.dynamic_slice_in_dim(matrix, head_index * DH, DH, 1)


def layer_norm(values, gain, shift):
    center = values - jnp.mean(values, -1, keepdims=True)
    spread = jnp.mean(center * center, -1, keepdims=True)
    return center * lax.rsqrt(spread + 1e-05) * gain + shift


def gelu_exact(values):
    return jax.nn.gelu(values, approximate=False)


def attend_forward(queries, keys_all, values_all, allowed):
    scaling = DH ** (-0.5)

    def one_head(head_index):
        scores = jnp.where(
            allowed,
            dot_second(column_slice(queries, head_index), column_slice(keys_all, head_index))
            * scaling,
            NEG_BIG,
        )
        largest = jnp.max(scores, 1, keepdims=True)
        expo = jnp.exp(scores - largest)
        total = jnp.sum(expo, 1, keepdims=True)
        probs = (expo / total).astype(jnp.bfloat16)
        return (
            dot_plain(probs, column_slice(values_all, head_index)),
            (largest + jnp.log(total))[:, 0],
        )

    heads, log_totals = lax.map(one_head, jnp.arange(HEADS))
    return (heads.transpose(1, 0, 2).reshape(queries.shape[0], HEADS * DH), log_totals)


def attend_backward(queries, keys_all, values_all, allowed, grad_att, log_totals):
    scaling = DH ** (-0.5)

    def one_head(item):
        head_index, log_row = item
        query_h = column_slice(queries, head_index)
        key_h = column_slice(keys_all, head_index)
        grad_h = column_slice(grad_att, head_index)
        scores = jnp.where(allowed, dot_second(query_h, key_h) * scaling, NEG_BIG)
        probs = jnp.exp(scores - log_row[:, None])
        grad_probs = dot_second(grad_h, column_slice(values_all, head_index))
        delta = jnp.sum(grad_probs * probs, 1, keepdims=True)
        grad_scores = (probs * (grad_probs - delta)).astype(jnp.bfloat16)
        grad_query = dot_plain(grad_scores, key_h) * scaling
        grad_key = dot_first(grad_scores, query_h) * scaling
        grad_value = dot_first(probs.astype(jnp.bfloat16), grad_h)
        return (grad_query, grad_key, grad_value)

    grad_q, grad_k, grad_v = lax.map(one_head, (jnp.arange(HEADS), log_totals))

    def merge_heads(block):
        return block.transpose(1, 0, 2).reshape(block.shape[1], HEADS * DH)

    return (merge_heads(grad_q), merge_heads(grad_k), merge_heads(grad_v))


def student_loss(stu_rows, pool_query, bias_pool, w_pool, w_class, bias_class, label_value):
    part_w = STU // SHEADS
    parts = stu_rows.reshape(stu_rows.shape[0], SHEADS, part_w)
    queries = pool_query.reshape(SHEADS, part_w)
    scores = jnp.einsum("tha,ha->ht", parts, queries, precision=HIGHEST) * part_w ** (-0.5)
    largest = jnp.max(scores, -1, keepdims=True)
    expo = jnp.exp(scores - largest)
    weights = expo / jnp.sum(expo, -1, keepdims=True)
    pooled = jnp.einsum("ht,tha->ha", weights, parts, precision=HIGHEST).reshape(STU)
    top_layer = jnp.tanh(jnp.dot(pooled, w_pool, precision=HIGHEST) + bias_pool)
    logit_row = jnp.dot(top_layer, w_class, precision=HIGHEST) + bias_class
    top_logit = jnp.max(logit_row)
    log_total = jnp.log(jnp.sum(jnp.exp(logit_row - top_logit))) + top_logit
    picked = jnp.sum(jnp.where(jnp.arange(logit_row.shape[0]) == label_value, logit_row, 0.0))
    return (log_total - picked, logit_row)


def body(
    prompt,
    conts,
    prompt_cot,
    cont_cot,
    labels,
    w_qkv,
    w_out,
    w_in,
    w_ffo,
    layer_biases,
    norm_gains,
    bias_in,
    w_student,
    student_vectors,
    w_pool,
    w_class,
    bias_class,
):
    prompt_rows = prompt.shape[1]
    cont_len = conts.shape[2]
    prompt_len = prompt_rows * lax.axis_size("shard")
    qkv_low = w_qkv.astype(jnp.bfloat16)
    out_low = w_out.astype(jnp.bfloat16)
    in_low = w_in.astype(jnp.bfloat16)
    ffo_low = w_ffo.astype(jnp.bfloat16)
    qkv_full, out_full, in_full, ffo_full = (
        lax.all_gather(qkv_low, "shard", axis=0, tiled=True),
        lax.all_gather(out_low, "shard", axis=0, tiled=True),
        lax.all_gather(in_low, "shard", axis=0, tiled=True),
        lax.all_gather(ffo_low, "shard", axis=0, tiled=True),
    )
    tokens = jnp.concatenate([prompt[0], conts[0, 0]], 0)
    tokens_f = tokens.astype(jnp.float32)
    zero_row = jnp.zeros((D,), jnp.float32)
    bias_three = jnp.concatenate([layer_biases[0], zero_row, layer_biases[1]])
    qkv_b = (dot_plain(tokens, qkv_full) + bias_three).astype(jnp.bfloat16)
    queries = qkv_b[:, :D]
    keys_own = qkv_b[:, D : 2 * D]
    values_own = qkv_b[:, 2 * D :]
    prompt_keys, prompt_values = (
        lax.all_gather(keys_own[:prompt_rows], "shard", axis=0, tiled=True),
        lax.all_gather(values_own[:prompt_rows], "shard", axis=0, tiled=True),
    )
    keys_all = jnp.concatenate([prompt_keys, keys_own[prompt_rows:]], 0)
    values_all = jnp.concatenate([prompt_values, values_own[prompt_rows:]], 0)
    key_pos = jnp.arange(prompt_len + cont_len)
    query_pos = jnp.concatenate(
        [
            lax.axis_index("shard") * prompt_rows + jnp.arange(prompt_rows),
            prompt_len + jnp.arange(cont_len),
        ]
    )
    allowed = key_pos[None, :] <= query_pos[:, None]
    attended, log_totals = attend_forward(queries, keys_all, values_all, allowed)
    att_b = attended.astype(jnp.bfloat16)
    branch = dot_plain(att_b, out_full) + layer_biases[2]
    resid_one = tokens_f + branch
    first = layer_norm(resid_one, norm_gains[0], layer_biases[4])
    first_b = first.astype(jnp.bfloat16)
    hidden = dot_plain(first_b, in_full) + bias_in
    act_b = gelu_exact(hidden).astype(jnp.bfloat16)
    ffn = dot_plain(act_b, ffo_full) + layer_biases[3]
    resid_two = first + ffn
    output = layer_norm(resid_two, norm_gains[1], layer_biases[5])
    output_b = output.astype(jnp.bfloat16)
    cont_b = output_b[prompt_rows:]
    student_low = w_student.astype(jnp.bfloat16)
    stu = dot_plain(cont_b, student_low) + student_vectors[0]

    def loss_closed(stu_rows, pool_query, bias_pool, pool_weight, class_weight, class_bias):
        return student_loss(
            stu_rows, pool_query, bias_pool, pool_weight, class_weight, class_bias, labels[0, 0]
        )

    loss_value, loss_pull, logit_row = jax.vjp(
        loss_closed,
        stu,
        student_vectors[1],
        student_vectors[2],
        w_pool,
        w_class,
        bias_class,
        has_aux=True,
    )
    g_stu, g_query, g_pbias, g_pool, g_class, g_cbias = loss_pull(jnp.ones((), jnp.float32))
    g_stu_b = g_stu.astype(jnp.bfloat16)
    g_sbias = jnp.sum(g_stu_b.astype(jnp.float32), 0)
    g_student = dot_first(cont_b, g_stu_b)
    student_back = dot_second(g_stu_b, student_low)
    g_output = jnp.concatenate([prompt_cot[0], cont_cot[0, 0]], 0).astype(jnp.float32)
    g_output = g_output + jnp.concatenate(
        [jnp.zeros((prompt_rows, D), jnp.float32), student_back], 0
    )
    qkv_back, out_back, in_back, ffo_back = (
        lax.all_gather(qkv_low, "shard", axis=0, tiled=True),
        lax.all_gather(out_low, "shard", axis=0, tiled=True),
        lax.all_gather(in_low, "shard", axis=0, tiled=True),
        lax.all_gather(ffo_low, "shard", axis=0, tiled=True),
    )
    norm_two, norm_two_pull = jax.vjp(layer_norm, resid_two, norm_gains[1], layer_biases[5])
    g_resid_two, g_gain_two, g_shift_two = norm_two_pull(g_output)
    g_ffn_b = g_resid_two.astype(jnp.bfloat16)
    g_ffo = dot_first(act_b, g_ffn_b)
    g_ffo_bias = jnp.sum(g_ffn_b.astype(jnp.float32), 0)
    g_act = dot_second(g_ffn_b, ffo_back)
    gelu_value, gelu_pull = jax.vjp(gelu_exact, hidden)
    g_hidden_b = gelu_pull(g_act)[0].astype(jnp.bfloat16)
    g_in = dot_first(first_b, g_hidden_b)
    g_in_bias = jnp.sum(g_hidden_b.astype(jnp.float32), 0)
    g_first = g_resid_two + dot_second(g_hidden_b, in_back)
    norm_one, norm_one_pull = jax.vjp(layer_norm, resid_one, norm_gains[0], layer_biases[4])
    g_resid_one, g_gain_one, g_shift_one = norm_one_pull(g_first)
    g_branch_b = g_resid_one.astype(jnp.bfloat16)
    g_outw = dot_first(att_b, g_branch_b)
    g_out_bias = jnp.sum(g_branch_b.astype(jnp.float32), 0)
    g_att_b = dot_second(g_branch_b, out_back).astype(jnp.bfloat16)
    g_query_rows, g_keys_all, g_values_all = attend_backward(
        queries, keys_all, values_all, allowed, g_att_b, log_totals
    )
    query_grad_b = g_query_rows.astype(jnp.bfloat16)
    cont_kv_b = jnp.concatenate([g_keys_all[prompt_len:], g_values_all[prompt_len:]], 1).astype(
        jnp.bfloat16
    )
    block_kv_b = jnp.concatenate([g_keys_all[:prompt_len], g_values_all[:prompt_len]], 1).astype(
        jnp.bfloat16
    )
    kv_weights = qkv_back[:, D:]
    g_query_w = dot_first(tokens, query_grad_b)
    g_kv_w = dot_first(tokens[prompt_rows:], cont_kv_b)
    g_tokens = g_resid_one + dot_second(query_grad_b, qkv_back[:, :D])
    cont_through = dot_second(cont_kv_b, kv_weights)
    kv_summed = lax.psum_scatter(
        block_kv_b.astype(jnp.float32).astype(jnp.bfloat16),
        "shard",
        scatter_dimension=0,
        tiled=True,
    ).astype(jnp.float32)
    g_kv_w = g_kv_w + lax.dot_general(
        tokens_f[:prompt_rows],
        kv_summed,
        (((0,), (0,)), ((), ())),
        precision=HIGHEST,
        preferred_element_type=jnp.float32,
    )
    prompt_through = jnp.dot(
        kv_summed,
        kv_weights.astype(jnp.float32).T,
        precision=HIGHEST,
        preferred_element_type=jnp.float32,
    )
    value_cols = jnp.sum(kv_summed[:, D:], 0)
    g_tokens = g_tokens + jnp.concatenate([prompt_through, cont_through], 0)
    g_qkvw = jnp.concatenate([g_query_w, g_kv_w], 1)
    g_query_bias = jnp.sum(query_grad_b.astype(jnp.float32), 0)
    g_value_bias = jnp.sum(cont_kv_b[:, D:].astype(jnp.float32), 0) + value_cols
    owned = (
        lax.psum_scatter(
            g_qkvw.astype(jnp.bfloat16), "shard", scatter_dimension=0, tiled=True
        ).astype(jnp.float32),
        lax.psum_scatter(
            g_outw.astype(jnp.bfloat16), "shard", scatter_dimension=0, tiled=True
        ).astype(jnp.float32),
        lax.psum_scatter(
            g_in.astype(jnp.bfloat16), "shard", scatter_dimension=0, tiled=True
        ).astype(jnp.float32),
        lax.psum_scatter(
            g_ffo.astype(jnp.bfloat16), "shard", scatter_dimension=0, tiled=True
        ).astype(jnp.float32),
    )
    owned_qkv, owned_out, owned_in, owned_ffo = (
        lax.psum(owned[0].astype(jnp.bfloat16), "rep").astype(jnp.float32),
        lax.psum(owned[1].astype(jnp.bfloat16), "rep").astype(jnp.float32),
        lax.psum(owned[2].astype(jnp.bfloat16), "rep").astype(jnp.float32),
        lax.psum(owned[3].astype(jnp.bfloat16), "rep").astype(jnp.float32),
    )
    g_biases = jnp.stack(
        [g_query_bias, g_value_bias, g_out_bias, g_ffo_bias, g_shift_one, g_shift_two]
    )
    g_gains = jnp.stack([g_gain_one, g_gain_two])
    g_vectors = jnp.stack([g_sbias, g_query, g_pbias])
    summed = lax.psum(
        (g_biases, g_gains, g_in_bias, g_student, g_vectors, g_pool, g_class, g_cbias),
        ("rep", "shard"),
    )
    return (
        output_b[:prompt_rows][None],
        output_b[prompt_rows:][None, None],
        logit_row[None, None],
        g_tokens[:prompt_rows][None],
        g_tokens[prompt_rows:][None, None],
        owned_qkv,
        owned_out,
        owned_in,
        owned_ffo,
        summed[0],
        summed[1],
        summed[2],
        summed[3],
        summed[4],
        summed[5],
        summed[6],
        summed[7],
    )


def solution(mesh):
    return jax.shard_map(
        body,
        mesh=mesh,
        in_specs=(
            P("rep", "shard", None),
            P("rep", "shard", None, None),
            P("rep", "shard", None),
            P("rep", "shard", None, None),
            P("rep", "shard"),
            P("shard", None),
            P("shard", None),
            P("shard", None),
            P("shard", None),
            P(),
            P(),
            P(),
            P(),
            P(),
            P(),
            P(),
            P(),
        ),
        out_specs=(
            P("rep", "shard", None),
            P("rep", "shard", None, None),
            P("rep", "shard", None),
            P("rep", "shard", None),
            P("rep", "shard", None, None),
            P("shard", None),
            P("shard", None),
            P("shard", None),
            P("shard", None),
            P(),
            P(),
            P(),
            P(),
            P(),
            P(),
            P(),
            P(),
        ),
        check_vma=False,
    )
```

profile of v0, /device:TPU:0, one launch (start us, length us, event | category | flops | bytes accessed | tf_op | source)
XLA Modules:
  0.0 1008.1 jit_solution(7969806802003201834)
XLA Ops:
  10.5 33.2 %all-gather.7.cloned.1.call-done = bf16[768,2304]{1,0:T(8,128)(2,1)} async-done(((bf16[192,2304]{1,0:T(8,128)(2,1)}), bf16[768,2304]{1,0:T(8,128)(2,1)}) %all-gather.7.cloned.1.call-update) | async-done | bytes 3538960 | tf_op jit(solution)/shard_map/all_gather | solution.py:140
  43.7 5.3 add_convert_fusion.1
  65.4 6.2 all-gather.11.cloned.1.call-done
  73.4 20.0 %all-gather.9.cloned.1.call-done = bf16[1024,768]{1,0:T(8,128)(2,1)} async-done(((bf16[256,768]{1,0:T(8,128)(2,1)}), bf16[1024,768]{1,0:T(8,128)(2,1)}) %all-gather.9.cloned.1.call-update) | async-done | bytes 1572880 | tf_op jit(solution)/shard_map/all_gather | solution.py:154
  97.8 133.8 %while.28 = (s32[]{:T(128)}, bf16[12,768,64]{1,2,0:T(8,128)(2,1)}, f32[12,768]{1,0:T(8,128)}, s32[12]{0:T(128)S(1)}, bf16[768,768]{1,0:T(8,128)(2,1)}, /*index=5...) while((s32[]{:T(128)}, bf16[12,768,64]{1,2,0:T(8,128)(2,1)}, ...), condition=%wide.region_3.4_spmd.clone, body=%wide.region_0.3_spmd.clone.sunk | while | flops 312605952 | bytes 34253524 | solution.py:66
  104.7 4.1 fusion.160
  115.8 4.1 fusion.160
  138.1 4.2 fusion.160
  149.2 4.1 fusion.160
  160.3 4.6 fusion.160
  171.9 4.1 fusion.160
  183.0 4.2 fusion.160
  194.1 4.1 fusion.160
  205.2 4.1 fusion.160
  216.3 4.1 fusion.160
  227.4 4.1 fusion.160
  236.9 29.4 %multiply_convert_fusion.1 = (bf16[768,3072]{1,0:T(8,128)(2,1)}, f32[768,3072]{1,0:T(8,128)}, f32[768,3072]{1,0:T(8,128)}) fusion(f32[3072]{0:T(1024)S(1)} %copy-done.42, bf16[768,3072]{1,0:T(8,128)(2,1)} %all-gather.15.cloned.1.call-done, f32[768,768]{0,1:T(8,128)S(1)} %get-tuple-element.319, f32[768]{0:T(1024)S(1)} %get-tuple-element.226, ...), kind=kOutput, calls=%fused_computation.48 | convolution fusion | flops 3782541312 | bytes 30695424 | tf_op jit(solution)/shard_map/dot_general | solution.py:18
  266.3 8.7 fusion.101
  294.4 13.0 %convert_reduce_fusion = (f32[3072]{0:T(1024)S(1)}, bf16[768,3072]{1,0:T(8,128)(2,1)S(1)}) fusion(f32[768,3072]{1,0:T(8,128)} %get-tuple-element.302, f32[768,3072]{1,0:T(8,128)} %get-tuple-element.320, f32[3072]{0:T(1024)S(1)} %copy-done.43, bf16[768,768]{0,1:T(8,128)(2,1)S(1)} %get-tuple-element.288, bf16[3072,768]{1,0:T(8,128)(2,1)} %all-gather.17.cloned.1.call-done), kind=kOutput, calls=%fused_computation.46 | convolution fusion | flops 3663983616 | bytes 29515776 | tf_op jit(solution)/shard_map/dot_general | solution.py:28
  307.5 4.5 multiply_reduce_fusion.2
  317.4 168.6 %while.29 = (s32[]{:T(128)}, bf16[12,768,64]{1,2,0:T(8,128)(2,1)}, bf16[12,1536,64]{1,2,0:T(8,128)(2,1)}, bf16[12,1536,64]{1,2,0:T(8,128)(2,1)}, s32[12]{0:T(128...) while((s32[]{:T(128)}, bf16[12,768,64]{1,2,0:T(8,128)(2,1)}, ...), condition=%wide.region_23.24_spmd.clone, body=%wide.region_21.23_spmd.clone.sunk | while | flops 766917888 | bytes 38360792 | solution.py:88
  497.0 32.6 %reduce-scatter.8.cloned.1.call-done = bf16[256,1536]{0,1:T(8,128)(2,1)} async-done(((bf16[1024,1536]{0,1:T(8,128)(2,1)}), bf16[256,1536]{0,1:T(8,128)(2,1)}) %reduce-scatter.8.cloned.1.call-update) | async-done | bytes 786448 | tf_op jit(solution)/shard_map/reduce_scatter | solution.py:245
  535.2 5.8 copy.89
  544.9 9.7 convolution_convert_fusion.1
  554.7 8.7 convolution_convert_fusion
  563.5 18.1 %reduce-scatter.16.cloned.1.call-done = bf16[192,2304]{1,0:T(8,128)(2,1)} async-done(((bf16[768,2304]{1,0:T(8,128)(2,1)}), bf16[192,2304]{1,0:T(8,128)(2,1)}) %reduce-scatter.16.cloned.1.call-update) | async-done | bytes 884752
  583.9 26.6 %reduce-scatter.10.cloned.1.call-done = bf16[192,768]{1,0:T(8,128)(2,1)} async-done(((bf16[768,768]{1,0:T(8,128)(2,1)}), bf16[192,768]{1,0:T(8,128)(2,1)}) %reduce-scatter.10.cloned.1.call-update) | async-done | bytes 294928 | tf_op jit(solution)/shard_map/reduce_scatter | solution.py:273
  610.5 50.4 %reduce-scatter.12.cloned.1.call-done = bf16[192,3072]{1,0:T(8,128)(2,1)} async-done(((bf16[768,3072]{1,0:T(8,128)(2,1)}), bf16[192,3072]{1,0:T(8,128)(2,1)}) %reduce-scatter.12.cloned.1.call-update) | async-done | bytes 1179664 | tf_op jit(solution)/shard_map/reduce_scatter | solution.py:276
  661.0 50.4 %reduce-scatter.14.cloned.1.call-done = bf16[768,768]{1,0:T(8,128)(2,1)} async-done(((bf16[3072,768]{1,0:T(8,128)(2,1)}), bf16[768,768]{1,0:T(8,128)(2,1)}) %reduce-scatter.14.cloned.1.call-update) | async-done | bytes 1179664 | tf_op jit(solution)/shard_map/reduce_scatter | solution.py:279
  737.0 43.9 %all-reduce.1 = (f32[6,768]{1,0:T(8,128)}, f32[2,768]{1,0:T(2,128)}, f32[3072]{0:T(1024)}, f32[3,128]{1,0:T(4,128)}, f32[128,14]{0,1:T(8,128)}, /*index=5*/f32[14]{0:T(128)}) all-reduce(f32[6,768]{1,0:T(8,128)S(1)} %stack.32, f32[2,768]{1,0:T(2,128)S(1)} %pad_maximum_fusion.11, ...), channel_id=1, replica_groups=mesh['rep'=8,'shard'=4] {'rep','shard'}, use_global_device_ids=true, to_apply=%region_40.41 | all-reduce | flops 11406 | bytes 91248 | tf_op jit(solution)/shard_map/psum | solution.py:294
  780.9 84.9 %all-reduce.9.cloned.1.call-done = (bf16[192,2304]{0,1:T(8,128)(2,1)}, bf16[192,768]{1,0:T(8,128)(2,1)}, bf16[192,3072]{1,0:T(8,128)(2,1)}, bf16[768,768]{1,0:T(8,128)(2,1)}) async-done(((bf16[192,2304]{0,1:T(8,128)(2,1)}, bf16[192,768]{1,0:T(8,128)(2,1)}, bf16[192,3072]{1,0:T(8,128)(2,1)}, bf16[768,768]{1,0:T(8,128)(2,1)}), (bf16[192,2304]{0,1:T(8,128)(2,1)}, bf16[192,768]{1,0:T(8,128)(2,1)}, ...) | async-done | bytes 3538960 | tf_op jit(solution)/shard_map/psum | solution.py:284
  872.9 125.0 %all-reduce.7.cloned.1.call-done = (f32[768,128]{1,0:T(8,128)}, f32[128,128]{1,0:T(8,128)}) async-done(((f32[768,128]{1,0:T(8,128)}, f32[128,128]{1,0:T(8,128)}), (f32[768,128]{1,0:T(8,128)}, f32[128,128]{1,0:T(8,128)})) %all-reduce.7.cloned.1.call-update) | async-done | bytes 458768 | tf_op jit(solution)/shard_map/psum | solution.py:294
  (439 shorter events, 351.7 us)
Async XLA Ops:
  7.2 272.0 %copy-start = (f32[128,128]{1,0:T(8,128)S(1)}, f32[128,128]{1,0:T(8,128)}, u32[]{:S(2)}) copy-start(f32[128,128]{1,0:T(8,128)} %param.35) | copy-start | bytes 196612
  7.2 36.5 %all-gather.7.cloned.1.call-start = ((), (), s32[]{:S(2)}) async-start(), calls=%async_computation.5 | async-start | bytes 4423680 | tf_op jit(solution)/shard_map/all_gather | solution.py:140
  9.9 61.7 %all-gather.11.cloned.1.call-start = ((), (), s32[]{:S(2)}) async-start(), calls=%async_computation.7 | async-start | bytes 1966080 | tf_op jit(solution)/shard_map/all_gather | solution.py:155
  10.2 33.5 %copy-start.27 = (bf16[1,1,512,768]{2,3,1,0:T(8,128)(2,1)}, bf16[1,1,512,768]{2,3,1,0:T(8,128)(2,1)S(1)}, u32[]{:S(2)}) copy-start(bf16[1,1,512,768]{2,3,1,0:T(8,128)(2,1)S(1)} %copy.63) | copy-start | bytes 2359300
  10.4 33.3 %copy-start.31 = (bf16[1,256,768]{1,2,0:T(8,128)(2,1)}, bf16[1,256,768]{1,2,0:T(8,128)(2,1)S(1)}, u32[]{:S(2)}) copy-start(bf16[1,256,768]{1,2,0:T(8,128)(2,1)S(1)} %copy.62) | copy-start | bytes 1179652
  43.7 8.8 copy-start.29
  51.8 41.7 %all-gather.9.cloned.1.call-start = ((), (), s32[]{:S(2)}) async-start(), calls=%async_computation.6 | async-start | bytes 1966080 | tf_op jit(solution)/shard_map/all_gather | solution.py:154
  52.5 179.0 %all-gather.13.cloned.1.call-start = ((), (), s32[]{:S(2)}) async-start(), calls=%async_computation.8 | async-start | bytes 1474560 | tf_op jit(solution)/shard_map/all_gather | solution.py:141
  53.3 183.1 %all-gather.15.cloned.1.call-start = ((), (), s32[]{:S(2)}) async-start(), calls=%async_computation.9 | async-start | bytes 5898240 | tf_op jit(solution)/shard_map/all_gather | solution.py:142
  54.6 4.5 copy-start.26
  54.6 4.8 copy-start.30
  54.6 211.6 %all-gather.17.cloned.1.call-start = ((), (), s32[]{:S(2)}) async-start(), calls=%async_computation.10 | async-start | bytes 5898240 | tf_op jit(solution)/shard_map/all_gather | solution.py:143
  57.6 472.1 %reduce-scatter.8.cloned.1.call-start = ((), (), s32[]{:S(2)}) async-start(), calls=%async_computation.11 | async-start | bytes 3932160 | tf_op jit(solution)/shard_map/reduce_scatter | solution.py:245
  236.1 30.1 %copy-start.6 = (f32[768,768]{0,1:T(8,128)}, f32[768,768]{0,1:T(8,128)S(1)}, u32[]{:S(2)}) copy-start(f32[768,768]{0,1:T(8,128)S(1)} %get-tuple-element.319) | copy-start | bytes 7077892
  275.3 4.0 copy-start.35
  280.7 4.5 copy-start.39
  287.6 4.3 copy-start.11
  293.7 13.7 %slice-start = ((s8[4718592]{0:T(1024)(128)(4,1)}), s8[4194304]{0:T(1024)(128)(4,1)S(1)}, s32[]{:S(2)}) async-start(s8[4718592]{0:T(1024)(128)(4,1)} %bitcast.224), calls=%async_computation.18 | async-start | bytes 8388608
  294.0 13.4 %copy-start.19 = (bf16[768,768]{0,1:T(8,128)(2,1)}, bf16[768,768]{0,1:T(8,128)(2,1)S(1)}, u32[]{:S(2)}) copy-start(bf16[768,768]{0,1:T(8,128)(2,1)S(1)} %get-tuple-element.288) | copy-start | bytes 3538948
  294.4 13.0 %copy-start.7 = (f32[768,768]{0,1:T(8,128)S(1)}, f32[768,768]{0,1:T(8,128)}, u32[]{:S(2)}) copy-start(f32[768,768]{0,1:T(8,128)} %copy-done.6) | copy-start | bytes 7077892
  294.4 13.1 %slice-start.1 = ((s8[4718592]{0:T(1024)(128)(4,1)}), s8[524288]{0:T(1024)(128)(4,1)S(1)}, s32[]{:S(2)}) async-start(s8[4718592]{0:T(1024)(128)(4,1)} %bitcast.224), calls=%async_computation.19 | async-start | bytes 1048576
  307.5 4.6 copy-start.44
  491.2 90.4 %reduce-scatter.16.cloned.1.call-start = ((), (), s32[]{:S(2)}) async-start(), calls=%async_computation.15 | async-start | bytes 4423680
  491.4 3.5 copy-start.4
  541.0 69.5 %reduce-scatter.10.cloned.1.call-start = ((), (), s32[]{:S(2)}) async-start(), calls=%async_computation.12 | async-start | bytes 1474560 | tf_op jit(solution)/shard_map/reduce_scatter | solution.py:273
  544.9 116.1 %reduce-scatter.12.cloned.1.call-start = ((), (), s32[]{:S(2)}) async-start(), calls=%async_computation.13 | async-start | bytes 5898240 | tf_op jit(solution)/shard_map/reduce_scatter | solution.py:276
  554.7 156.7 %reduce-scatter.14.cloned.1.call-start = ((), (), s32[]{:S(2)}) async-start(), calls=%async_computation.14 | async-start | bytes 5898240 | tf_op jit(solution)/shard_map/reduce_scatter | solution.py:279
  563.5 302.3 %all-reduce.9.cloned.1.call-start = ((), (), s32[]{:S(2)}) async-start(), calls=%async_computation.17 | async-start | bytes 7667712 | tf_op jit(solution)/shard_map/psum | solution.py:284
  711.4 286.5 %all-reduce.7.cloned.1.call-start = ((), (), s32[]{:S(2)}) async-start(), calls=%async_computation.16 | async-start | bytes 917504 | tf_op jit(solution)/shard_map/psum | solution.py:294
  716.0 7.0 copy-start.24
  725.3 3.6 copy-start.33
  870.5 130.7 %copy-start.1 = (f32[128,128]{1,0:T(8,128)S(1)}, f32[128,128]{1,0:T(8,128)}, u32[]{:S(2)}) copy-start(f32[128,128]{1,0:T(8,128)} %param.35) | copy-start | bytes 196612
  (39 other events, 83.0 us)
Sparse Core Ops, SparseCore 0:
  10.2 33.4 all-gather.6
  51.9 19.6 all-gather.10
  73.7 19.6 all-gather.8
  95.4 17.4 all-gather.12
  114.9 37.4 all-gather.14
  153.8 37.4 all-gather.16
  491.3 38.3 reduce-scatter.7
  541.2 40.4 reduce-scatter.15
  584.8 25.7 reduce-scatter.9
  613.1 47.8 reduce-scatter.11
  663.5 47.8 reduce-scatter.13
  716.4 149.4 all-reduce.8
  872.6 125.2 all-reduce.6
where the time goes:
time: 1020 us; the launch traced here: 1010 us
  waiting for transfers between devices  448 us (44%)
  matrix products  322 us (32%)
  local copies, waits for them, and re-layouts  108 us (11%)
  other arithmetic  50.7 us (5%)
  blocking collectives  43.9 us (4%)
  between operations  17.9 us (2%)
  loops' own time  16.2 us (2%)
    dot_general x29, matrix products, dot_plain(): return jnp.dot(left, right, preferred_element_type=jnp.float32)  127 us
    psum x1, waiting for transfers between devices, body(): lax.psum((g_biases, g_gains, g_in_bias, g_student, g_vectors, g_pool, g_c...  125 us
    dot_general x42, matrix products, dot_second(): lax.dot_general(left, right, (((1,), (1,)), ((), ())), preferred_element_...  107 us
    psum x1, waiting for transfers between devices, body(): lax.psum(owned[0].astype(jnp.bfloat16), 'rep').astype(jnp.float32)  84.9 us
    dot_general x30, matrix products, dot_first(): lax.dot_general(left, right, (((0,), (0,)), ((), ())), preferred_element_...  82.1 us
    reduce_scatter x1, waiting for transfers between devices, body(): lax.psum_scatter(g_ffo.astype(jnp.bfloat16), 'shard', scatter_dimension=0...  50.4 us
    reduce_scatter x1, waiting for transfers between devices, body(): lax.psum_scatter(g_in.astype(jnp.bfloat16), 'shard', scatter_dimension=0,...  50.4 us
    psum x1, blocking collectives, body(): lax.psum((g_biases, g_gains, g_in_bias, g_student, g_vectors, g_pool, g_c...  43.9 us
  transfers between devices with their start and end apart: 13, of which 10 were waited for; matrix products, arithmetic and copies ran while one was open for 22% of the time, Pallas kernels for 0%

commit v1 on v0

--- a/solution.py
+++ b/solution.py
@@ -1,6 +1,8 @@
 import jax
 import jax.numpy as jnp
 from jax import lax
+from jax.experimental import pallas as pl
+from jax.experimental.pallas import tpu as pltpu
 from jax.sharding import PartitionSpec as P
 
 D = 768
@@ -30,10 +32,6 @@
     )
 
 
-def column_slice(matrix, head_index):
-    return lax.dynamic_slice_in_dim(matrix, head_index * DH, DH, 1)
-
-
 def layer_norm(values, gain, shift):
     center = values - jnp.mean(values, -1, keepdims=True)
     spread = jnp.mean(center * center, -1, keepdims=True)
@@ -44,53 +42,533 @@
     return jax.nn.gelu(values, approximate=False)
 
 
-def attend_forward(queries, keys_all, values_all, allowed):
-    scaling = DH ** (-0.5)
-
-    def one_head(head_index):
-        scores = jnp.where(
-            allowed,
-            dot_second(column_slice(queries, head_index), column_slice(keys_all, head_index))
-            * scaling,
-            NEG_BIG,
+TILE = 256
+PAIR = 128
+VMEM_ALL = 60 * 1024 * 1024
+
+
+def rows_dot(left, right):
+    return lax.dot_general(
+        left, right, (((1,), (1,)), ((), ())), preferred_element_type=jnp.float32
+    )
+
+
+def low_lanes(shape):
+    return lax.broadcasted_iota(jnp.int32, shape, len(shape) - 1) < DH
+
+
+def attend_fwd_pair(shard, prompt_rows, q, kp, vp, kc, vc, att_ref, lse_ref):
+    cont_len = kc.shape[0]
+    prompt_len = kp.shape[0]
+    for start in range(0, prompt_rows + cont_len, TILE):
+        q_t = q[start : start + TILE, :] * jnp.asarray(DH ** (-0.5), jnp.bfloat16)
+        halves = []
+        for parity in range(2):
+            keep = low_lanes(q_t.shape) == (parity == 0)
+            q_h = jnp.where(keep, q_t, jnp.zeros_like(q_t))
+            s_p = rows_dot(q_h, kp[...])
+            if start < prompt_rows:
+                key = lax.broadcasted_iota(jnp.int32, s_p.shape, 1)
+                row = lax.broadcasted_iota(jnp.int32, s_p.shape, 0)
+                s_p = jnp.where(key <= row + (shard * prompt_rows + start), s_p, NEG_BIG)
+                largest = jnp.max(s_p, 1, keepdims=True)
+                p_p = jnp.exp(s_p - largest)
+                total = jnp.sum(p_p, 1, keepdims=True)
+                o = dot_plain(p_p.astype(jnp.bfloat16), vp[...])
+            else:
+                seen = start - prompt_rows + TILE
+                s_c = rows_dot(q_h, kc[:seen, :])
+                key = lax.broadcasted_iota(jnp.int32, s_c.shape, 1)
+                row = lax.broadcasted_iota(jnp.int32, s_c.shape, 0)
+                s_c = jnp.where(key <= row + (start - prompt_rows), s_c, NEG_BIG)
+                largest = jnp.maximum(
+                    jnp.max(s_p, 1, keepdims=True), jnp.max(s_c, 1, keepdims=True)
+                )
+                p_p = jnp.exp(s_p - largest)
+                p_c = jnp.exp(s_c - largest)
+                total = jnp.sum(p_p, 1, keepdims=True) + jnp.sum(p_c, 1, keepdims=True)
+                o = dot_plain(p_p.astype(jnp.bfloat16), vp[...]) + dot_plain(
+                    p_c.astype(jnp.bfloat16), vc[:seen, :]
+                )
+            halves.append((o / total, largest + jnp.log(total)))
+        keep = low_lanes((TILE, PAIR))
+        att_ref[start : start + TILE, :] = jnp.where(keep, halves[0][0], halves[1][0])
+        lse = jnp.where(
+            keep,
+            jnp.broadcast_to(halves[0][1], (TILE, PAIR)),
+            jnp.broadcast_to(halves[1][1], (TILE, PAIR)),
         )
-        largest = jnp.max(scores, 1, keepdims=True)
-        expo = jnp.exp(scores - largest)
-        total = jnp.sum(expo, 1, keepdims=True)
-        probs = (expo / total).astype(jnp.bfloat16)
-        return (
-            dot_plain(probs, column_slice(values_all, head_index)),
-            (largest + jnp.log(total))[:, 0],
+        turned = jnp.transpose(lse)
+        lse_ref[0:1, start : start + TILE] = turned[0:1, :]
+        lse_ref[1:2, start : start + TILE] = turned[DH : DH + 1, :]
+
+
+def attend_bwd_pair(
+    shard, prompt_rows, q, kp, vp, kc, vc, g, att, lse, dq, dkp, dvp, dkc, dvc, accum
+):
+    cont_len = kc.shape[0]
+    tokens = prompt_rows + cont_len
+    prompt_len = kp.shape[0]
+    g_t = g[...]
+    turned = jnp.transpose(g_t.astype(jnp.float32) * att[...])
+    delta = (
+        jnp.sum(turned[:DH], 0, keepdims=True),
+        jnp.sum(turned[DH:], 0, keepdims=True),
+    )
+    q_t = q[...] * jnp.asarray(DH ** (-0.5), jnp.bfloat16)
+    keep = low_lanes(q_t.shape)
+    zero = jnp.zeros_like(q_t)
+    q_h = (jnp.where(keep, q_t, zero), jnp.where(keep, zero, q_t))
+    g_h = (jnp.where(keep, g_t, zero), jnp.where(keep, zero, g_t))
+    accum[...] = jnp.zeros_like(accum)
+
+    def block(key_b, value_b, first, mask):
+        key_t = jnp.transpose(key_b.astype(jnp.float32)).astype(jnp.bfloat16)
+        g_key = jnp.zeros((TILE, PAIR), jnp.float32)
+        g_value = jnp.zeros((TILE, PAIR), jnp.float32)
+        for parity in range(2):
+            scores = rows_dot(key_b, q_h[parity][first:])
+            probs = jnp.exp(scores - lse[parity : parity + 1, first:])
+            masked = jnp.where(mask, probs[:, :TILE], 0.0)
+            if tokens - first > TILE:
+                probs = jnp.concatenate([masked, probs[:, TILE:]], 1)
+            else:
+                probs = masked
+            g_probs = rows_dot(value_b, g_h[parity][first:])
+            g_scores = (probs * (g_probs - delta[parity][:, first:])).astype(jnp.bfloat16)
+            g_value += dot_plain(probs.astype(jnp.bfloat16), g_h[parity][first:])
+            g_key += dot_plain(g_scores, q_h[parity][first:])
+            rows = slice(parity * DH, (parity + 1) * DH)
+            accum[rows, first:] += dot_plain(key_t[rows], g_scores)
+        return g_key.astype(jnp.bfloat16), g_value.astype(jnp.bfloat16)
+
+    ahead = lax.broadcasted_iota(jnp.int32, (TILE, TILE), 0) - lax.broadcasted_iota(
+        jnp.int32, (TILE, TILE), 1
+    )
+
+    def prompt_block(index, start):
+        rows = pl.ds(start, TILE)
+        mask = ahead <= shard * prompt_rows - index * TILE
+        g_key, g_value = block(kp[rows, :], vp[rows, :], 0, mask)
+        dkp[rows, :] = g_key
+        dvp[rows, :] = g_value
+
+    blocks = prompt_len // TILE
+    if blocks <= 4:
+        for index in range(blocks):
+            prompt_block(index, index * TILE)
+    else:
+
+        def step(index, carry):
+            prompt_block(index, pl.multiple_of(index * TILE, TILE))
+            return carry
+
+        lax.fori_loop(0, blocks, step, 0)
+    for start in range(0, cont_len, TILE):
+        rows = slice(start, start + TILE)
+        g_key, g_value = block(kc[rows, :], vc[rows, :], prompt_rows + start, ahead <= 0)
+        dkc[rows, :] = g_key
+        dvc[rows, :] = g_value
+    dq[...] = (jnp.transpose(accum[...]) * DH ** (-0.5)).astype(jnp.bfloat16)
+
+
+def attend_forward(qkv_b, kv_prompt, prompt_rows):
+    tokens = qkv_b.shape[0]
+    prompt_len = kv_prompt.shape[0]
+    cont_len = tokens - prompt_rows
+    pairs = HEADS // 2
+
+    def kernel(q, kp, vp, ko, vo, att_ref, lse_ref):
+        attend_fwd_pair(
+            lax.axis_index("shard"),
+            prompt_rows,
+            q,
+            kp,
+            vp,
+            ko.at[prompt_rows:, :],
+            vo.at[prompt_rows:, :],
+            att_ref,
+            lse_ref.at[0],
         )
 
-    heads, log_totals = lax.map(one_head, jnp.arange(HEADS))
-    return (heads.transpose(1, 0, 2).reshape(queries.shape[0], HEADS * DH), log_totals)
-
-
-def attend_backward(queries, keys_all, values_all, allowed, grad_att, log_totals):
-    scaling = DH ** (-0.5)
-
-    def one_head(item):
-        head_index, log_row = item
-        query_h = column_slice(queries, head_index)
-        key_h = column_slice(keys_all, head_index)
-        grad_h = column_slice(grad_att, head_index)
-        scores = jnp.where(allowed, dot_second(query_h, key_h) * scaling, NEG_BIG)
-        probs = jnp.exp(scores - log_row[:, None])
-        grad_probs = dot_second(grad_h, column_slice(values_all, head_index))
-        delta = jnp.sum(grad_probs * probs, 1, keepdims=True)
-        grad_scores = (probs * (grad_probs - delta)).astype(jnp.bfloat16)
-        grad_query = dot_plain(grad_scores, key_h) * scaling
-        grad_key = dot_first(grad_scores, query_h) * scaling
-        grad_value = dot_first(probs.astype(jnp.bfloat16), grad_h)
-        return (grad_query, grad_key, grad_value)
-
-    grad_q, grad_k, grad_v = lax.map(one_head, (jnp.arange(HEADS), log_totals))
-
-    def merge_heads(block):
-        return block.transpose(1, 0, 2).reshape(block.shape[1], HEADS * DH)
-
-    return (merge_heads(grad_q), merge_heads(grad_k), merge_heads(grad_v))
+    return pl.pallas_call(
+        kernel,
+        grid=(pairs,),
+        in_specs=[
+            pl.BlockSpec((tokens, PAIR), lambda p: (0, p)),
+            pl.BlockSpec((prompt_len, PAIR), lambda p: (0, p)),
+            pl.BlockSpec((prompt_len, PAIR), lambda p: (0, pairs + p)),
+            pl.BlockSpec((tokens, PAIR), lambda p: (0, pairs + p)),
+            pl.BlockSpec((tokens, PAIR), lambda p: (0, 2 * pairs + p)),
+        ],
+        out_specs=[
+            pl.BlockSpec((tokens, PAIR), lambda p: (0, p)),
+            pl.BlockSpec((1, 8, tokens), lambda p: (p, 0, 0)),
+        ],
+        out_shape=[
+            jax.ShapeDtypeStruct((tokens, D), jnp.float32),
+            jax.ShapeDtypeStruct((pairs, 8, tokens), jnp.float32),
+        ],
+        compiler_params=pltpu.CompilerParams(vmem_limit_bytes=VMEM_ALL),
+        name="attend_forward",
+    )(qkv_b, kv_prompt, kv_prompt, qkv_b, qkv_b)
+
+
+def attend_backward(qkv_b, kv_prompt, g_att, att, lse, prompt_rows):
+    tokens = qkv_b.shape[0]
+    prompt_len = kv_prompt.shape[0]
+    cont_len = tokens - prompt_rows
+    pairs = HEADS // 2
+
+    def kernel(q, kp, vp, ko, vo, g, a, ls, dq, dkp, dvp, dkc, dvc, accum):
+        attend_bwd_pair(
+            lax.axis_index("shard"),
+            prompt_rows,
+            q,
+            kp,
+            vp,
+            ko.at[prompt_rows:, :],
+            vo.at[prompt_rows:, :],
+            g,
+            a,
+            ls.at[0],
+            dq,
+            dkp,
+            dvp,
+            dkc,
+            dvc,
+            accum,
+        )
+
+    def columns(rows):
+        return pl.BlockSpec((rows, PAIR), lambda p: (0, p))
+
+    return pl.pallas_call(
+        kernel,
+        grid=(pairs,),
+        in_specs=[
+            columns(tokens),
+            columns(prompt_len),
+            pl.BlockSpec((prompt_len, PAIR), lambda p: (0, pairs + p)),
+            pl.BlockSpec((tokens, PAIR), lambda p: (0, pairs + p)),
+            pl.BlockSpec((tokens, PAIR), lambda p: (0, 2 * pairs + p)),
+            columns(tokens),
+            columns(tokens),
+            pl.BlockSpec((1, 8, tokens), lambda p: (p, 0, 0)),
+        ],
+        out_specs=[
+            columns(tokens),
+            columns(prompt_len),
+            columns(prompt_len),
+            columns(cont_len),
+            columns(cont_len),
+        ],
+        out_shape=[
+            jax.ShapeDtypeStruct((tokens, D), jnp.bfloat16),
+            jax.ShapeDtypeStruct((prompt_len, D), jnp.bfloat16),
+            jax.ShapeDtypeStruct((prompt_len, D), jnp.bfloat16),
+            jax.ShapeDtypeStruct((cont_len, D), jnp.bfloat16),
+            jax.ShapeDtypeStruct((cont_len, D), jnp.bfloat16),
+        ],
+        scratch_shapes=[pltpu.VMEM((PAIR, tokens), jnp.float32)],
+        compiler_params=pltpu.CompilerParams(vmem_limit_bytes=VMEM_ALL),
+        name="attend_backward",
+    )(qkv_b, kv_prompt, kv_prompt, qkv_b, qkv_b, g_att, att, lse)
+
+
+MESH_ID = pl.DeviceIdType.MESH
+
+
+def sum_gradients(g_qkv, g_out, g_in, g_ffo, g_small):
+    pieces = 12
+    rows = g_qkv.shape[0] // 4
+    width, half, quarter = D, D // 2, rows // 4
+    s_width, s_half = g_small.shape[1], g_small.shape[1] // 2
+    ahead = 3
+
+    def kernel(
+        gq, go, gi, gf, gs, out, out_s,
+        own, cr, xs, xr, yb, yr, zb, zr, fb,
+        own_s, cr_s, xs_s, xr_s, yb_s, yr_s, zb_s, zr_s, fb_s,
+        sem_own, c_send, c_recv, x_send, x_recv, y_send, y_recv, z_send, z_recv,
+        f_send, f_recv, o_send, o_recv, o_own, g_send, g_recv,
+    ):
+        rep, shard = lax.axis_index("rep"), lax.axis_index("shard")
+        z, y = rep // 2, rep % 2
+        x, core = shard // 2, shard % 2
+        partner = (rep, 2 * x + 1 - core)
+        across = (rep, 2 * (1 - x) + core)
+        beside = (2 * z + 1 - y, shard)
+
+        def along(step):
+            return (2 * lax.rem(z + step, 4) + y, shard)
+
+        barrier = pltpu.get_barrier_semaphore()
+        others = [partner, across, beside, along(1), along(2), along(3)]
+        far = (rep, 2 * (1 - x) + 1 - core)
+        for other in others + [far]:
+            pl.semaphore_signal(barrier, inc=1, device_id=other, device_id_type=MESH_ID)
+        pl.semaphore_wait(barrier, len(others) + 1)
+
+        def remote(source, target, send, recv, device):
+            return pltpu.make_async_remote_copy(
+                src_ref=source,
+                dst_ref=target,
+                send_sem=send,
+                recv_sem=recv,
+                device_id=device,
+                device_id_type=MESH_ID,
+            )
+
+        def source(k, block):
+            if k < 4:
+                return gf.at[pl.ds(block * 4 * rows + k * rows, rows), :]
+            if k < 8:
+                return gi.at[pl.ds(block * rows, rows), (k - 4) * width : (k - 3) * width]
+            if k < 9:
+                return go.at[pl.ds(block * rows, rows), :]
+            if k < 12:
+                return gq.at[pl.ds(block * rows, rows), (k - 9) * width : (k - 8) * width]
+            return gs.at[pl.ds(block * rows, rows), :]
+
+        big = (own, cr, xs, xr, yb, yr, zb, zr, fb, half)
+        small = (own_s, cr_s, xs_s, xr_s, yb_s, yr_s, zb_s, zr_s, fb_s, s_half)
+
+        def bufs(k):
+            if isinstance(k, int) and k == pieces:
+                return small, 0
+            return big, k
+
+        def core_copy(k, xx):
+            b, i = bufs(k)
+            return remote(
+                source(k, 2 * xx + 1 - core) if isinstance(k, int) else b[1].at[i, xx],
+                b[1].at[i, xx],
+                c_send.at[k, xx],
+                c_recv.at[k, xx],
+                partner,
+            )
+
+        def own_copy(k, xx):
+            b, i = bufs(k)
+            return pltpu.make_async_copy(
+                source(k, 2 * xx + core) if isinstance(k, int) else b[0].at[i, xx],
+                b[0].at[i, xx],
+                sem_own.at[k, xx],
+            )
+
+        def x_copy(k):
+            b, i = bufs(k)
+            return remote(b[2].at[i], b[3].at[i], x_send.at[k], x_recv.at[k], across)
+
+        def y_copy(k):
+            b, i = bufs(k)
+            return remote(b[4].at[i, 1 - y], b[5].at[i], y_send.at[k], y_recv.at[k], beside)
+
+        def z_copy(k, step, buf, slot, send, recv, target):
+            return remote(buf, target, send.at[k, step - 1], recv.at[k, slot], along(step))
+
+        def zs_copy(k, step):
+            b, i = bufs(k)
+            return z_copy(
+                k, step, b[6].at[i, lax.rem(z + step, 4)], z, z_send, z_recv, b[7].at[i, z]
+            )
+
+        def zr_wait(k, step):
+            b, i = bufs(k)
+            slot = lax.rem(z + step, 4)
+            z_copy(k, step, b[7].at[i, slot], slot, z_send, z_recv, b[7].at[i, slot]).wait_recv()
+
+        def fs_copy(k, step):
+            b, i = bufs(k)
+            return z_copy(k, step, b[8].at[i, z], z, f_send, f_recv, b[8].at[i, z])
+
+        def fr_wait(k, step):
+            b, i = bufs(k)
+            slot = lax.rem(z + step, 4)
+            z_copy(k, step, b[8].at[i, slot], slot, f_send, f_recv, b[8].at[i, slot]).wait_recv()
+
+        def final(k, yy):
+            if isinstance(k, int) and k == pieces:
+                return out_s.at[shard, :, :, pl.ds(pl.multiple_of(yy * s_half, 128), s_half)]
+            return out.at[k, :, :, pl.ds(pl.multiple_of(yy * half, 128), half)]
+
+        def o_copy(k):
+            b, i = bufs(k)
+            return remote(b[8].at[i], final(k, y), o_send.at[k], o_recv.at[k], beside)
+
+        def o_wait(k):
+            b, i = bufs(k)
+            remote(b[8].at[i], final(k, 1 - y), o_send.at[k], o_recv.at[k], beside).wait_recv()
+
+        def o_local(k):
+            b, i = bufs(k)
+            return pltpu.make_async_copy(b[8].at[i], final(k, y), o_own.at[k])
+
+        def wide(value):
+            return value.astype(jnp.float32)
+
+        def stage_x(k):
+            b, i = bufs(k)
+            for xx in range(2):
+                core_copy(k, xx).wait_recv()
+                own_copy(k, xx).wait()
+            b[2][i] = (wide(b[0][i, 1 - x]) + wide(b[1][i, 1 - x])).astype(jnp.bfloat16)
+            x_copy(k).start()
+
+        def stage_y(k):
+            b, i = bufs(k)
+            x_copy(k).wait_recv()
+            total = (wide(b[0][i, x]) + wide(b[1][i, x]) + wide(b[3][i])).astype(jnp.bfloat16)
+            cut = b[9]
+            b[4][i, 0] = total[:, :cut]
+            b[4][i, 1] = total[:, cut:]
+            y_copy(k).start()
+
+        def stage_z(k):
+            b, i = bufs(k)
+            y_copy(k).wait_recv()
+            total = (wide(b[4][i, y]) + wide(b[5][i])).astype(jnp.bfloat16)
+            for q in range(4):
+                b[6][i, q] = total[q * quarter : (q + 1) * quarter]
+            for step in (2, 1, 3):
+                zs_copy(k, step).start()
+
+        def stage_f(k):
+            b, i = bufs(k)
+            total = wide(b[6][i, z])
+            for step in (1, 2, 3):
+                zr_wait(k, step)
+                total += wide(b[7][i, lax.rem(z + step, 4)])
+            b[8][i, z] = total.astype(jnp.bfloat16)
+            for step in (2, 1, 3):
+                fs_copy(k, step).start()
+
+        def stage_o(k):
+            for step in (1, 2, 3):
+                fr_wait(k, step)
+            o_copy(k).start()
+            o_local(k).start()
+
+        def g_copy(step):
+            return remote(
+                out_s.at[shard],
+                out_s.at[shard],
+                g_send.at[step - 1],
+                g_recv.at[shard],
+                (rep, lax.rem(shard + step, 4)),
+            )
+
+        def stage_g():
+            o_wait(pieces)
+            o_local(pieces).wait()
+            for step in (1, 2, 3):
+                g_copy(step).start()
+
+        order = [pieces] + list(range(pieces))
+        for k in order:
+            for xx in range(2):
+                core_copy(k, xx).start()
+                own_copy(k, xx).start()
+        stage_x(pieces)
+        for k in range(ahead):
+            stage_x(k)
+        small_stages = [stage_y, stage_z, stage_f, stage_o]
+
+        def tick(t, carry):
+            @pl.when(t + ahead < pieces)
+            def _():
+                stage_x(t + ahead)
+
+            for at, stage in enumerate(small_stages):
+
+                @pl.when(t == at)
+                def _(stage=stage):
+                    stage(pieces)
+
+            @pl.when(t == len(small_stages))
+            def _():
+                stage_g()
+
+            @pl.when(t < pieces)
+            def _():
+                stage_y(t)
+
+            for late, stage in ((1, stage_z), (2, stage_f), (3, stage_o)):
+
+                @pl.when((t >= late) & (t < pieces + late))
+                def _(late=late, stage=stage):
+                    stage(t - late)
+
+            return carry
+
+        lax.fori_loop(0, pieces + 3, tick, 0)
+
+        def finish(k):
+            for xx in range(2):
+                core_copy(k, xx).wait_send()
+            x_copy(k).wait_send()
+            y_copy(k).wait_send()
+            for step in (1, 2, 3):
+                zs_copy(k, step).wait_send()
+                fs_copy(k, step).wait_send()
+            o_copy(k).wait_send()
+
+        def last(k, carry):
+            o_wait(k)
+            o_local(k).wait()
+            finish(k)
+            return carry
+
+        lax.fori_loop(0, pieces, last, 0)
+        finish(pieces)
+        for step in (1, 2, 3):
+            slot = lax.rem(shard + step, 4)
+            remote(
+                out_s.at[slot], out_s.at[slot], g_send.at[step - 1], g_recv.at[slot], far
+            ).wait_recv()
+            g_copy(step).wait_send()
+
+    def buffers(count, wide_cols):
+        cut = wide_cols // 2
+        return [
+            pltpu.VMEM((count, 2, rows, wide_cols), jnp.bfloat16),
+            pltpu.VMEM((count, 2, rows, wide_cols), jnp.bfloat16),
+            pltpu.VMEM((count, rows, wide_cols), jnp.bfloat16),
+            pltpu.VMEM((count, rows, wide_cols), jnp.bfloat16),
+            pltpu.VMEM((count, 2, rows, cut), jnp.bfloat16),
+            pltpu.VMEM((count, rows, cut), jnp.bfloat16),
+            pltpu.VMEM((count, 4, quarter, cut), jnp.bfloat16),
+            pltpu.VMEM((count, 4, quarter, cut), jnp.bfloat16),
+            pltpu.VMEM((count, 4, quarter, cut), jnp.bfloat16),
+        ]
+
+    def sems(*dims):
+        return pltpu.SemaphoreType.DMA(dims)
+
+    n = pieces + 1
+    anywhere = pl.BlockSpec(memory_space=pl.ANY)
+    out, out_s = pl.pallas_call(
+        kernel,
+        in_specs=[anywhere] * 5,
+        out_specs=[anywhere, pl.BlockSpec(memory_space=pltpu.VMEM)],
+        out_shape=[
+            jax.ShapeDtypeStruct((pieces, 4, quarter, width), jnp.bfloat16),
+            jax.ShapeDtypeStruct((4, 4, quarter, s_width), jnp.bfloat16),
+        ],
+        scratch_shapes=buffers(pieces, width)
+        + buffers(1, s_width)
+        + [
+            sems(n, 2), sems(n, 2), sems(n, 2), sems(n), sems(n), sems(n), sems(n),
+            sems(n, 3), sems(n, 4), sems(n, 3), sems(n, 4), sems(n), sems(n), sems(n),
+            sems(3), sems(4),
+        ],
+        compiler_params=pltpu.CompilerParams(
+            collective_id=0, has_side_effects=True, vmem_limit_bytes=VMEM_ALL
+        ),
+        name="sum_gradients",
+    )(g_qkv, g_out, g_in, g_ffo, g_small)
+    return out.reshape(pieces, rows, width), out_s.reshape(4 * rows, s_width)
 
 
 def student_loss(stu_rows, pool_query, bias_pool, w_pool, w_class, bias_class, label_value):
@@ -108,6 +586,57 @@
     log_total = jnp.log(jnp.sum(jnp.exp(logit_row - top_logit))) + top_logit
     picked = jnp.sum(jnp.where(jnp.arange(logit_row.shape[0]) == label_value, logit_row, 0.0))
     return (log_total - picked, logit_row)
+
+
+def sum_native(g_qkvw, g_outw, g_in, g_ffo, small):
+    def over(grad):
+        part = lax.psum_scatter(
+            grad.astype(jnp.bfloat16), "shard", scatter_dimension=0, tiled=True
+        )
+        return lax.psum(part, "rep").astype(jnp.float32)
+
+    owned = tuple(over(grad) for grad in (g_qkvw, g_outw, g_in, g_ffo))
+    return owned, lax.psum(small, ("rep", "shard"))
+
+
+def sum_direct(g_qkvw, g_outw, g_in, g_ffo, small):
+    biases, gains, in_bias, student, vectors, pool, class_w, class_b = small
+    parts = [
+        biases.reshape(-1, 128),
+        gains.reshape(-1, 128),
+        in_bias.reshape(-1, 128),
+        vectors.reshape(-1, 128),
+        pool.reshape(-1, 128),
+        jnp.pad(class_w, ((0, 0), (0, 128 - class_w.shape[1]))),
+        jnp.pad(class_b[None], ((0, 0), (0, 128 - class_b.shape[0]))),
+    ]
+    used = sum(part.shape[0] for part in parts)
+    side = jnp.concatenate(parts + [jnp.zeros((D - used, 128), jnp.float32)], 0)
+    packed = jnp.concatenate([student, side], 1).astype(jnp.bfloat16)
+    low = [grad.astype(jnp.bfloat16) for grad in (g_qkvw, g_outw, g_in, g_ffo)]
+    out, summed = sum_gradients(*low, packed)
+    out = out.astype(jnp.float32)
+    summed = summed.astype(jnp.float32)
+    owned = (
+        jnp.concatenate([out[9], out[10], out[11]], 1),
+        out[8],
+        jnp.concatenate([out[4], out[5], out[6], out[7]], 1),
+        out[:4].reshape(-1, D),
+    )
+    result, at = [summed[:, :128]], 0
+    for part in parts:
+        result.append(summed[at : at + part.shape[0], 128:])
+        at += part.shape[0]
+    return owned, (
+        result[1].reshape(biases.shape),
+        result[2].reshape(gains.shape),
+        result[3].reshape(in_bias.shape),
+        result[0],
+        result[4].reshape(vectors.shape),
+        result[5].reshape(pool.shape),
+        result[6][:, : class_w.shape[1]],
+        result[7][0, : class_b.shape[0]],
+    )
 
 
 def body(
@@ -147,24 +676,8 @@
     zero_row = jnp.zeros((D,), jnp.float32)
     bias_three = jnp.concatenate([layer_biases[0], zero_row, layer_biases[1]])
     qkv_b = (dot_plain(tokens, qkv_full) + bias_three).astype(jnp.bfloat16)
-    queries = qkv_b[:, :D]
-    keys_own = qkv_b[:, D : 2 * D]
-    values_own = qkv_b[:, 2 * D :]
-    prompt_keys, prompt_values = (
-        lax.all_gather(keys_own[:prompt_rows], "shard", axis=0, tiled=True),
-        lax.all_gather(values_own[:prompt_rows], "shard", axis=0, tiled=True),
-    )
-    keys_all = jnp.concatenate([prompt_keys, keys_own[prompt_rows:]], 0)
-    values_all = jnp.concatenate([prompt_values, values_own[prompt_rows:]], 0)
-    key_pos = jnp.arange(prompt_len + cont_len)
-    query_pos = jnp.concatenate(
-        [
-            lax.axis_index("shard") * prompt_rows + jnp.arange(prompt_rows),
-            prompt_len + jnp.arange(cont_len),
-        ]
-    )
-    allowed = key_pos[None, :] <= query_pos[:, None]
-    attended, log_totals = attend_forward(queries, keys_all, values_all, allowed)
+    kv_prompt = lax.all_gather(qkv_b[:prompt_rows, D:], "shard", axis=0, tiled=True)
+    attended, log_totals = attend_forward(qkv_b, kv_prompt, prompt_rows)
     att_b = attended.astype(jnp.bfloat16)
     branch = dot_plain(att_b, out_full) + layer_biases[2]
     resid_one = tokens_f + branch
@@ -227,23 +740,18 @@
     g_outw = dot_first(att_b, g_branch_b)
     g_out_bias = jnp.sum(g_branch_b.astype(jnp.float32), 0)
     g_att_b = dot_second(g_branch_b, out_back).astype(jnp.bfloat16)
-    g_query_rows, g_keys_all, g_values_all = attend_backward(
-        queries, keys_all, values_all, allowed, g_att_b, log_totals
-    )
-    query_grad_b = g_query_rows.astype(jnp.bfloat16)
-    cont_kv_b = jnp.concatenate([g_keys_all[prompt_len:], g_values_all[prompt_len:]], 1).astype(
-        jnp.bfloat16
-    )
-    block_kv_b = jnp.concatenate([g_keys_all[:prompt_len], g_values_all[:prompt_len]], 1).astype(
-        jnp.bfloat16
-    )
+    query_grad_b, g_keys_p, g_values_p, g_keys_c, g_values_c = attend_backward(
+        qkv_b, kv_prompt, g_att_b, attended, log_totals, prompt_rows
+    )
+    cont_kv_b = jnp.concatenate([g_keys_c, g_values_c], 1)
+    block_kv_b = jnp.concatenate([g_keys_p, g_values_p], 1)
     kv_weights = qkv_back[:, D:]
     g_query_w = dot_first(tokens, query_grad_b)
     g_kv_w = dot_first(tokens[prompt_rows:], cont_kv_b)
     g_tokens = g_resid_one + dot_second(query_grad_b, qkv_back[:, :D])
     cont_through = dot_second(cont_kv_b, kv_weights)
     kv_summed = lax.psum_scatter(
-        block_kv_b.astype(jnp.float32).astype(jnp.bfloat16),
+        block_kv_b,
         "shard",
         scatter_dimension=0,
         tiled=True,
@@ -266,35 +774,15 @@
     g_qkvw = jnp.concatenate([g_query_w, g_kv_w], 1)
     g_query_bias = jnp.sum(query_grad_b.astype(jnp.float32), 0)
     g_value_bias = jnp.sum(cont_kv_b[:, D:].astype(jnp.float32), 0) + value_cols
-    owned = (
-        lax.psum_scatter(
-            g_qkvw.astype(jnp.bfloat16), "shard", scatter_dimension=0, tiled=True
-        ).astype(jnp.float32),
-        lax.psum_scatter(
-            g_outw.astype(jnp.bfloat16), "shard", scatter_dimension=0, tiled=True
-        ).astype(jnp.float32),
-        lax.psum_scatter(
-            g_in.astype(jnp.bfloat16), "shard", scatter_dimension=0, tiled=True
-        ).astype(jnp.float32),
-        lax.psum_scatter(
-            g_ffo.astype(jnp.bfloat16), "shard", scatter_dimension=0, tiled=True
-        ).astype(jnp.float32),
-    )
-    owned_qkv, owned_out, owned_in, owned_ffo = (
-        lax.psum(owned[0].astype(jnp.bfloat16), "rep").astype(jnp.float32),
-        lax.psum(owned[1].astype(jnp.bfloat16), "rep").astype(jnp.float32),
-        lax.psum(owned[2].astype(jnp.bfloat16), "rep").astype(jnp.float32),
-        lax.psum(owned[3].astype(jnp.bfloat16), "rep").astype(jnp.float32),
-    )
     g_biases = jnp.stack(
         [g_query_bias, g_value_bias, g_out_bias, g_ffo_bias, g_shift_one, g_shift_two]
     )
     g_gains = jnp.stack([g_gain_one, g_gain_two])
     g_vectors = jnp.stack([g_sbias, g_query, g_pbias])
-    summed = lax.psum(
-        (g_biases, g_gains, g_in_bias, g_student, g_vectors, g_pool, g_class, g_cbias),
-        ("rep", "shard"),
-    )
+    small = (g_biases, g_gains, g_in_bias, g_student, g_vectors, g_pool, g_class, g_cbias)
+    direct = (lax.axis_size("rep"), lax.axis_size("shard")) == (8, 4)
+    owned, summed = (sum_direct if direct else sum_native)(g_qkvw, g_outw, g_in, g_ffo, small)
+    owned_qkv, owned_out, owned_in, owned_ffo = owned
     return (
         output_b[:prompt_rows][None],
         output_b[prompt_rows:][None, None],

time: 1020 us -> 477 us (0.47)
  waiting for transfers between devices: 448 us -> 99.3 us
  matrix products: 322 us -> 102 us
  Pallas kernels: 0 us -> 177 us
  local copies, waits for them, and re-layouts: 108 us -> 37.5 us
  blocking collectives: 43.9 us -> 0 us
  loops' own time: 16.2 us -> 0 us
  other arithmetic: 50.7 us -> 35.5 us
    psum x2 -> x0, waiting for transfers between devices: 210 us -> none  [the longest x1 125 us: body(): lax.psum((g_biases, g_gains, g_in_bias, g_student, g_vectors, g_pool, g_c...]
    pallas_call x0 -> x3, Pallas kernels: none -> 177 us  [the longest x1 115 us: sum_gradients(): pl.pallas_call(kernel, in_specs=[anywhere] * 5, out_specs=[anywhere, pl.B...]
    reduce_scatter x4 -> x1, waiting for transfers between devices: 160 us -> 3.85 us  [body(): lax.psum_scatter(block_kv_b, 'shard', scatter_dimension=0, tiled=True)]
    dot_general x29 -> x5, matrix products: 127 us -> 47.2 us  [dot_plain(): return jnp.dot(left, right, preferred_element_type=jnp.float32)]
    dot_general x42 -> x6, matrix products: 107 us -> 30 us  [dot_second(): lax.dot_general(left, right, (((1,), (1,)), ((), ())), preferred_element_...]
    dot_general x30 -> x6, matrix products: 82.1 us -> 18.7 us  [dot_first(): lax.dot_general(left, right, (((0,), (0,)), ((), ())), preferred_element_...]
    psum x1 -> x0, blocking collectives: 43.9 us -> none  [body(): lax.psum((g_biases, g_gains, g_in_bias, g_student, g_vectors, g_pool, g_c...]
    all_gather x1, waiting for transfers between devices: 0.02 us -> 30.8 us  [body(): lax.all_gather(in_low, 'shard', axis=0, tiled=True)]
  transfers between devices with their start and end apart: 13 -> 6, of which waited for: 10 -> 5; matrix products, arithmetic and copies ran while one was open for 22% -> 15% of each run, Pallas kernels for 0% -> 5%
where the time goes in v1:
time: 477 us; the launch traced here: 470 us
  Pallas kernels  177 us (37%)
  matrix products  102 us (21%)
  waiting for transfers between devices  99.3 us (21%)
  local copies, waits for them, and re-layouts  37.5 us (8%)
  other arithmetic  35.5 us (7%)
  between operations  18.2 us (4%)
    pallas_call x1, Pallas kernels, sum_gradients(): pl.pallas_call(kernel, in_specs=[anywhere] * 5, out_specs=[anywhere, pl.B...  115 us
    dot_general x5, matrix products, dot_plain(): return jnp.dot(left, right, preferred_element_type=jnp.float32)  47.2 us
    pallas_call x1, Pallas kernels, attend_backward(): pl.pallas_call(kernel, grid=(pairs,), in_specs=[columns(tokens), columns(...  38 us
    all_gather x1, waiting for transfers between devices, body(): lax.all_gather(qkv_low, 'shard', axis=0, tiled=True)  33.2 us
    all_gather x1, waiting for transfers between devices, body(): lax.all_gather(in_low, 'shard', axis=0, tiled=True)  30.8 us
    dot_general x6, matrix products, dot_second(): lax.dot_general(left, right, (((1,), (1,)), ((), ())), preferred_element_...  30 us
    pallas_call x1, Pallas kernels, attend_forward(): pl.pallas_call(kernel, grid=(pairs,), in_specs=[pl.BlockSpec((tokens, PAI...  24.5 us
    all_gather x1, waiting for transfers between devices, body(): lax.all_gather(qkv_b[:prompt_rows, D:], 'shard', axis=0, tiled=True)  21.4 us
  transfers between devices with their start and end apart: 6, of which 5 were waited for; matrix products, arithmetic and copies ran while one was open for 15% of the time, Pallas kernels for 5%

profile of v1, /device:TPU:0, one launch (start us, length us, event | category | flops | bytes accessed | tf_op | source)
XLA Modules:
  0.0 470.0 jit_solution(16328767311208600868)
XLA Ops:
  7.3 2.6 convert_element_type.108
  10.5 33.2 %all-gather.6.cloned.1.call-done = bf16[768,2304]{1,0:T(8,128)(2,1)} async-done(((bf16[192,2304]{1,0:T(8,128)(2,1)}), bf16[768,2304]{1,0:T(8,128)(2,1)}) %all-gather.6.cloned.1.call-update) | async-done | bytes 3538960 | tf_op jit(solution)/shard_map/all_gather | solution.py:669
  43.7 5.3 %add_convert_fusion.1.q.ko.vo = bf16[768,2304]{1,0:T(8,128)(2,1)S(1)} fusion(bf16[768,2304]{1,0:T(8,128)(2,1)} %all-gather.6.cloned.1.call-done, f32[2304]{0:T(1024)S(1)} %pad_maximum_fusion.8, bf16[512,768]{0,1:T(8,128)(2,1)S(1)} %bitcast.170, bf16[256,768]{0,1:T(8,128)(2,1)S(1)} %bitcast.176), kind=kOutput, calls=%fused_computation.17 | convolution fusion | flops 2723807232 | bytes 8266752 | tf_op jit(solution)/shard_map/dot_general | solution.py:20
  54.1 2.9 convert_element_type.115
  59.2 21.4 %all-gather.8.cloned.1.call-done.kp.vp = bf16[1024,1536]{1,0:T(8,128)(2,1)} async-done(((bf16[256,1536]{1,0:T(8,128)(2,1)}), bf16[1024,1536]{1,0:T(8,128)(2,1)}) %all-gather.8.cloned.1.call-update) | async-done | bytes 3145744 | tf_op jit(solution)/shard_map/all_gather | solution.py:679
  80.5 24.5 %attend_forward.1 = (f32[768,768]{1,0:T(8,128)}, f32[6,8,768]{2,1,0:T(8,128)}) custom-call(bf16[768,2304]{1,0:T(8,128)(2,1)} %copy-done.2, bf16[1024,1536]{1,0:T(8,128)(2,1)} %all-gather.8.cloned.1.call-done.kp.vp, bf16[1024,1536]{1,0:T(8,128)(2,1)} %all-gather.8.cloned.1.call-done.kp.vp, bf16[768,2304]{1,0:T(8,128)(2,1)} %copy-done.2, ...), custom_call_target="tpu_custom_call" | custom-call | tf_op jit(solution)/shard_map/attend_forward/pallas_call | solution.py:194
  105.0 3.5 fusion.64
  108.9 30.8 %all-gather.12.cloned.1.call-done = bf16[768,3072]{1,0:T(8,128)(2,1)} async-done(((bf16[192,3072]{1,0:T(8,128)(2,1)}), bf16[768,3072]{1,0:T(8,128)(2,1)}) %all-gather.12.cloned.1.call-update) | async-done | bytes 4718608 | tf_op jit(solution)/shard_map/all_gather | solution.py:671
  139.6 29.4 %multiply_convert_fusion = (bf16[768,3072]{1,0:T(8,128)(2,1)}, f32[768,3072]{1,0:T(8,128)}, f32[768,3072]{1,0:T(8,128)}) fusion(f32[3072]{0:T(1024)S(1)} %copy-done.58, bf16[768,3072]{1,0:T(8,128)(2,1)} %all-gather.12.cloned.1.call-done, f32[768,768]{0,1:T(8,128)S(1)} %get-tuple-element.136, f32[768]{0:T(1024)S(1)} %get-tuple-element.93, ...), kind=kOutput, calls=%fused_computation.3 | convolution fusion | flops 3782541312 | bytes 30695424 | tf_op jit(solution)/shard_map/dot_general | solution.py:20
  169.1 10.0 %all-gather.14.cloned.1.call-done = bf16[3072,768]{1,0:T(8,128)(2,1)} async-done(((bf16[768,768]{1,0:T(8,128)(2,1)}), bf16[3072,768]{1,0:T(8,128)(2,1)}) %all-gather.14.cloned.1.call-update) | async-done | bytes 4718608 | tf_op jit(solution)/shard_map/all_gather | solution.py:672
  179.1 8.7 %fusion.65 = (f32[768]{0:T(1024)S(1)}, f32[768,768]{0,1:T(8,128)S(1)}) fusion(f32[768]{0:T(1024)S(1)} %get-tuple-element.97, bf16[768,3072]{1,0:T(8,128)(2,1)} %get-tuple-element.120, bf16[3072,768]{1,0:T(8,128)(2,1)} %all-gather.14.cloned.1.call-done, f32[768]{0:T(1024)S(1)} %get-tuple-element.93, f32[768]{0:T(1024)S(1)} %get-tuple-element.99, ...), kind=kOutput, calls=%fused_computation.160 | convolution fusion | flops 3628006656 | bytes 14174208 | tf_op jit(solution)/shard_map/dot_general | solution.py:20
  205.9 14.5 %fusion.54 = (bf16[3072]{0:T(1024)(128)(2,1)S(1)}, bf16[768,3072]{1,0:T(8,128)(2,1)}) fusion(f32[768,3072]{1,0:T(8,128)} %get-tuple-element.121, f32[768,3072]{1,0:T(8,128)} %get-tuple-element.137, f32[3072]{0:T(1024)S(1)} %copy-done.59, bf16[768,768]{0,1:T(8,128)(2,1)S(1)} %get-tuple-element.107, bf16[3072,768]{1,0:T(8,128)(2,1)} %all-gather.14.cloned.1.call-done), kind=kOutput, calls=%fused_computation.151 | convolution fusion | flops 3661624320 | bytes 29509632 | tf_op jit(solution)/shard_map/dot_general | solution.py:30
  220.4 7.0 %multiply_reduce_fusion.1 = (bf16[768]{0:T(1024)(128)(2,1)S(1)}, f32[768]{0:T(1024)S(1)}, bf16[768]{0:T(1024)(128)(2,1)S(1)}, f32[768,768]{0,1:T(8,128)S(1)}) fusion(f32[768,768]{0,1:T(8,128)S(1)} %copy-done.5, f32[768]{0:T(1024)S(1)} %fusion.36, f32[768]{0:T(1024)S(1)} %broadcast_multiply_fusion.1, f32[768]{0:T(1024)S(1)} %get-tuple-element.99, ...), kind=kOutput, calls=%fused_computation.29 | convolution fusion | flops 3629774592 | bytes 16533504 | tf_op jit(solution)/shard_map/dot_general | solution.py:30
  229.4 2.2 convolution_convert_fusion.4.g
  231.5 38.0 %attend_backward.1 = (bf16[768,768]{1,0:T(8,128)(2,1)}, bf16[1024,768]{1,0:T(8,128)(2,1)}, bf16[1024,768]{1,0:T(8,128)(2,1)}, bf16[512,768]{1,0:T(8,128)(2,1)}, bf16[512,768]{1,0:T(8,128)(2,1)}) custom-call(bf16[768,2304]{1,0:T(8,128)(2,1)} %copy-done.2, bf16[1024,1536]{1,0:T(8,128)(2,1)} %all-gather.8.cloned.1.call-done.kp.vp, ...), custom_call_target="tpu_custom_call" | custom-call | tf_op jit(solution)/shard_map/attend_backward/pallas_call | solution.py:246
  269.6 3.7 pad_maximum_fusion.1
  278.7 1.9 slice_bitcast_fusion.3
  280.6 2.0 copy.85
  287.7 2.1 convolution_convert_fusion.3
  289.9 2.2 convolution_convert_fusion.2.go
  293.2 2.6 fusion.7
  295.8 5.7 %convolution_convert_fusion.gf = bf16[3072,768]{1,0:T(8,128)(2,1)} fusion(bf16[768,3072]{1,0:T(8,128)(2,1)S(1)} %bitcast.192, bf16[768,768]{0,1:T(8,128)(2,1)S(1)} %copy-done.29), kind=kOutput, calls=%fused_computation.18 | convolution fusion | flops 3626237952 | bytes 10616832 | tf_op jit(solution)/shard_map/dot_general | solution.py:24
  301.5 6.1 %convolution_convert_fusion.1.gi = bf16[768,3072]{1,0:T(8,128)(2,1)} fusion(bf16[768,3072]{1,0:T(8,128)(2,1)S(1)} %bitcast.190, f32[768,768]{0,1:T(8,128)S(1)} %copy-done.6, f32[768]{0:T(1024)S(1)} %copy-done.50, f32[768]{0:T(1024)S(1)} %get-tuple-element.99, f32[768]{0:T(1024)S(1)} %fusion.36, f32[768]{0:T(1024)S(1)} %broadcast_multiply_fusion.1), kind=kOutput, calls=%fused_computation.19 | convolution fusion | flops 3629187072 | bytes 11808768 | tf_op jit(solution)/shard_map/dot_general | solution.py:24
  307.6 3.9 reduce-scatter.2.cloned.1.call-done
  311.4 2.8 fusion.9
  314.3 2.5 maximum_add_fusion
  321.6 2.5 concatenate.47
  325.9 3.3 pad_maximum_fusion.gq
  329.1 114.8 %sum_gradients.1 = (bf16[12,4,48,768]{3,2,1,0:T(8,128)(2,1)}, bf16[4,4,48,256]{3,2,1,0:T(8,128)(2,1)}) custom-call(bf16[768,2304]{1,0:T(8,128)(2,1)} %pad_maximum_fusion.gq, bf16[768,768]{1,0:T(8,128)(2,1)} %convolution_convert_fusion.2.go, bf16[768,3072]{1,0:T(8,128)(2,1)} %convolution_convert_fusion.1.gi, bf16[3072,768]{1,0:T(8,128)(2,1)} %convolution_convert_fusion.gf, ...), custom_call_target="tpu_custom_call" | custom-call | tf_op jit(solution)/shard_map/sum_gradients/pallas_call | solution.py:551
  448.1 3.1 slice.181
  451.2 2.0 fusion.63
  458.2 2.7 pad_maximum_fusion.3
  (257 shorter events, 54.2 us)
Async XLA Ops:
  7.2 185.4 %copy-start = (f32[128,128]{1,0:T(8,128)S(1)}, f32[128,128]{1,0:T(8,128)}, u32[]{:S(2)}) copy-start(f32[128,128]{1,0:T(8,128)} %param.31) | copy-start | bytes 196612
  7.2 36.5 %all-gather.6.cloned.1.call-start = ((), (), s32[]{:S(2)}) async-start(), calls=%async_computation.1 | async-start | bytes 4423680 | tf_op jit(solution)/shard_map/all_gather | solution.py:669
  9.9 70.6 %all-gather.8.cloned.1.call-start = ((), (), s32[]{:S(2)}) async-start(), calls=%async_computation.2 | async-start | bytes 3932160 | tf_op jit(solution)/shard_map/all_gather | solution.py:679
  10.1 33.6 %copy-start.39 = (bf16[1,256,768]{1,2,0:T(8,128)(2,1)}, bf16[1,256,768]{1,2,0:T(8,128)(2,1)S(1)}, u32[]{:S(2)}) copy-start(bf16[1,256,768]{1,2,0:T(8,128)(2,1)S(1)} %copy.70) | copy-start | bytes 1179652
  10.4 33.3 %copy-start.33 = (bf16[1,1,512,768]{2,3,1,0:T(8,128)(2,1)}, bf16[1,1,512,768]{2,3,1,0:T(8,128)(2,1)S(1)}, u32[]{:S(2)}) copy-start(bf16[1,1,512,768]{2,3,1,0:T(8,128)(2,1)S(1)} %copy.71) | copy-start | bytes 2359300
  10.5 168.6 %copy-start.49 = (f32[768]{0:T(1024)}, f32[768]{0:T(1024)S(1)}, u32[]{:S(2)}) copy-start(f32[768]{0:T(1024)S(1)} %get-tuple-element.93) | copy-start | bytes 9220
  43.7 8.2 %copy-start.35 = (f32[192,768]{1,0:T(8,128)S(1)}, f32[192,768]{1,0:T(8,128)}, u32[]{:S(2)}) copy-start(f32[192,768]{1,0:T(8,128)} %param.23) | copy-start | bytes 1769476
  51.8 53.2 %all-gather.10.cloned.1.call-start = ((), (), s32[]{:S(2)}) async-start(), calls=%async_computation.3 | async-start | bytes 1474560 | tf_op jit(solution)/shard_map/all_gather | solution.py:670
  52.7 87.0 %all-gather.12.cloned.1.call-start = ((), (), s32[]{:S(2)}) async-start(), calls=%async_computation.4 | async-start | bytes 5898240 | tf_op jit(solution)/shard_map/all_gather | solution.py:671
  54.0 4.8 %copy-start.32 = (bf16[1,1,512,768]{3,2,1,0:T(8,128)(2,1)S(1)}, bf16[1,1,512,768]{3,2,1,0:T(8,128)(2,1)}, u32[]{:S(2)}) copy-start(bf16[1,1,512,768]{3,2,1,0:T(8,128)(2,1)} %param.20) | copy-start | bytes 2359300
  54.1 125.1 %all-gather.14.cloned.1.call-start = ((), (), s32[]{:S(2)}) async-start(), calls=%async_computation.5 | async-start | bytes 5898240 | tf_op jit(solution)/shard_map/all_gather | solution.py:672
  57.0 254.4 %reduce-scatter.2.cloned.1.call-start = ((), (), s32[]{:S(2)}) async-start(), calls=%async_computation.6 | async-start | bytes 3932160 | tf_op jit(solution)/shard_map/reduce_scatter | solution.py:753
  57.8 144.0 %copy-start.47 = (f32[2,64]{1,0:T(2,128)}, f32[2,64]{1,0:T(2,128)S(1)}, u32[]{:S(2)}) copy-start(f32[2,64]{1,0:T(2,128)S(1)} %reshape_squeeze.3) | copy-start | bytes 1540
  108.5 60.5 %copy-start.4 = (f32[768,768]{0,1:T(8,128)}, f32[768,768]{0,1:T(8,128)S(1)}, u32[]{:S(2)}) copy-start(f32[768,768]{0,1:T(8,128)S(1)} %get-tuple-element.136) | copy-start | bytes 7077892
  108.6 31.1 %copy-start.58 = (f32[3072]{0:T(1024)S(1)}, f32[3072]{0:T(1024)}, u32[]{:S(2)}) copy-start(f32[3072]{0:T(1024)} %param.28) | copy-start | bytes 36868
  188.1 4.6 copy-start.55
  193.5 10.9 %copy-start.45 = (f32[14]{0:T(128)}, f32[14]{0:T(128)S(1)}, u32[]{:S(2)}) copy-start(f32[14]{0:T(128)S(1)} %get-tuple-element.141) | copy-start | bytes 172
  205.2 15.2 %slice-start = ((s8[4718592]{0:T(1024)(128)(4,1)}), s8[4194304]{0:T(1024)(128)(4,1)S(1)}, s32[]{:S(2)}) async-start(s8[4718592]{0:T(1024)(128)(4,1)} %bitcast.187), calls=%async_computation.7 | async-start | bytes 8388608
  205.5 14.9 %copy-start.28 = (bf16[768,768]{0,1:T(8,128)(2,1)}, bf16[768,768]{0,1:T(8,128)(2,1)S(1)}, u32[]{:S(2)}) copy-start(bf16[768,768]{0,1:T(8,128)(2,1)S(1)} %get-tuple-element.107) | copy-start | bytes 3538948
  205.9 14.5 %copy-start.5 = (f32[768,768]{0,1:T(8,128)S(1)}, f32[768,768]{0,1:T(8,128)}, u32[]{:S(2)}) copy-start(f32[768,768]{0,1:T(8,128)} %copy-done.4) | copy-start | bytes 7077892
  205.9 14.5 %slice-start.1 = ((s8[4718592]{0:T(1024)(128)(4,1)}), s8[524288]{0:T(1024)(128)(4,1)S(1)}, s32[]{:S(2)}) async-start(s8[4718592]{0:T(1024)(128)(4,1)} %bitcast.187), calls=%async_computation.8 | async-start | bytes 1048576
  278.7 6.9 %copy-start.17 = (bf16[512,768]{1,0:T(8,128)(2,1)S(1)}, bf16[512,768]{1,0:T(8,128)(2,1)}, u32[]{:S(2)}) copy-start(bf16[512,768]{1,0:T(8,128)(2,1)} %get-tuple-element.32) | copy-start | bytes 2359300
  285.7 6.3 %copy-start.13 = (bf16[512,1536]{1,0:T(8,128)(2,1)}, bf16[512,1536]{1,0:T(8,128)(2,1)S(1)}, u32[]{:S(2)}) copy-start(bf16[512,1536]{1,0:T(8,128)(2,1)S(1)} %constant_dynamic-update-slice_fusion) | copy-start | bytes 4718596
  287.7 8.0 %slice-start.4 = ((s8[4718592]{0:T(1024)(128)(4,1)}), s8[4194304]{0:T(1024)(128)(4,1)S(1)}, s32[]{:S(2)}) async-start(s8[4718592]{0:T(1024)(128)(4,1)} %bitcast.191), calls=%async_computation.11 | async-start | bytes 8388608
  289.9 5.9 %slice-start.5 = ((s8[4718592]{0:T(1024)(128)(4,1)}), s8[524288]{0:T(1024)(128)(4,1)S(1)}, s32[]{:S(2)}) async-start(s8[4718592]{0:T(1024)(128)(4,1)} %bitcast.191), calls=%async_computation.12 | async-start | bytes 1048576
  293.2 8.3 %slice-start.2 = ((s8[4718592]{0:T(1024)(128)(4,1)}), s8[4194304]{0:T(1024)(128)(4,1)S(1)}, s32[]{:S(2)}) async-start(s8[4718592]{0:T(1024)(128)(4,1)} %bitcast.189), calls=%async_computation.9 | async-start | bytes 8388608
  295.7 5.7 %copy-start.6 = (f32[768,768]{0,1:T(8,128)S(1)}, f32[768,768]{0,1:T(8,128)}, u32[]{:S(2)}) copy-start(f32[768,768]{0,1:T(8,128)} %copy-done.4) | copy-start | bytes 7077892
  295.7 5.7 %copy-start.50 = (f32[768]{0:T(1024)S(1)}, f32[768]{0:T(1024)}, u32[]{:S(2)}) copy-start(f32[768]{0:T(1024)} %copy-done.49) | copy-start | bytes 9220
  295.8 5.7 %slice-start.3 = ((s8[4718592]{0:T(1024)(128)(4,1)}), s8[524288]{0:T(1024)(128)(4,1)S(1)}, s32[]{:S(2)}) async-start(s8[4718592]{0:T(1024)(128)(4,1)} %bitcast.189), calls=%async_computation.10 | async-start | bytes 1048576
  455.2 5.8 %copy-start.19 = (f32[1,4,48,768]{3,2,1,0:T(8,128)S(1)}, f32[1,4,48,768]{3,2,1,0:T(8,128)}, u32[]{:S(2)}) copy-start(f32[1,4,48,768]{3,2,1,0:T(8,128)} %get-tuple-element.123) | copy-start | bytes 1769476
  455.2 5.8 %copy-start.20 = (f32[1,4,48,768]{3,2,1,0:T(8,128)S(1)}, f32[1,4,48,768]{3,2,1,0:T(8,128)}, u32[]{:S(2)}) copy-start(f32[1,4,48,768]{3,2,1,0:T(8,128)} %get-tuple-element.124) | copy-start | bytes 1769476
  456.4 4.6 copy-start.21
  (40 other events, 96.8 us)
Sparse Core Ops, SparseCore 0:
  10.2 33.4 all-gather.5
  51.9 28.5 all-gather.7
  82.7 17.4 all-gather.9
  102.1 37.4 all-gather.11
  141.6 37.4 all-gather.13
  273.5 37.9 reduce-scatter.1

commit v2 on v1

--- a/solution.py
+++ b/solution.py
@@ -57,7 +57,9 @@
     return lax.broadcasted_iota(jnp.int32, shape, len(shape) - 1) < DH
 
 
-def attend_fwd_pair(shard, prompt_rows, q, kp, vp, kc, vc, att_ref, lse_ref):
+def attend_fwd_pair(
+    shard, prompt_rows, q, kp, vp, kc, vc, att_ref, lse_ref, between=None
+):
     cont_len = kc.shape[0]
     prompt_len = kp.shape[0]
     for start in range(0, prompt_rows + cont_len, TILE):
@@ -101,6 +103,8 @@
         turned = jnp.transpose(lse)
         lse_ref[0:1, start : start + TILE] = turned[0:1, :]
         lse_ref[1:2, start : start + TILE] = turned[DH : DH + 1, :]
+        if between is not None:
+            between(start // TILE)
 
 
 def attend_bwd_pair(
@@ -172,63 +176,45 @@
     dq[...] = (jnp.transpose(accum[...]) * DH ** (-0.5)).astype(jnp.bfloat16)
 
 
-def attend_forward(qkv_b, kv_prompt, prompt_rows):
-    tokens = qkv_b.shape[0]
-    prompt_len = kv_prompt.shape[0]
-    cont_len = tokens - prompt_rows
+def attend_forward(q, kp, vp, kc, vc, prompt_rows):
+    tokens, prompt_len, cont_len = q.shape[0], kp.shape[0], kc.shape[0]
     pairs = HEADS // 2
 
-    def kernel(q, kp, vp, ko, vo, att_ref, lse_ref):
+    def kernel(q, kp, vp, kc, vc, att_ref, lse_ref):
         attend_fwd_pair(
-            lax.axis_index("shard"),
-            prompt_rows,
-            q,
-            kp,
-            vp,
-            ko.at[prompt_rows:, :],
-            vo.at[prompt_rows:, :],
-            att_ref,
-            lse_ref.at[0],
+            lax.axis_index("shard"), prompt_rows, q, kp, vp, kc, vc, att_ref, lse_ref.at[0]
         )
+
+    def columns(rows):
+        return pl.BlockSpec((rows, PAIR), lambda p: (0, p))
 
     return pl.pallas_call(
         kernel,
         grid=(pairs,),
-        in_specs=[
-            pl.BlockSpec((tokens, PAIR), lambda p: (0, p)),
-            pl.BlockSpec((prompt_len, PAIR), lambda p: (0, p)),
-            pl.BlockSpec((prompt_len, PAIR), lambda p: (0, pairs + p)),
-            pl.BlockSpec((tokens, PAIR), lambda p: (0, pairs + p)),
-            pl.BlockSpec((tokens, PAIR), lambda p: (0, 2 * pairs + p)),
-        ],
-        out_specs=[
-            pl.BlockSpec((tokens, PAIR), lambda p: (0, p)),
-            pl.BlockSpec((1, 8, tokens), lambda p: (p, 0, 0)),
-        ],
+        in_specs=[columns(rows) for rows in (tokens, prompt_len, prompt_len, cont_len, cont_len)],
+        out_specs=[columns(tokens), pl.BlockSpec((1, 8, tokens), lambda p: (p, 0, 0))],
         out_shape=[
             jax.ShapeDtypeStruct((tokens, D), jnp.float32),
             jax.ShapeDtypeStruct((pairs, 8, tokens), jnp.float32),
         ],
         compiler_params=pltpu.CompilerParams(vmem_limit_bytes=VMEM_ALL),
         name="attend_forward",
-    )(qkv_b, kv_prompt, kv_prompt, qkv_b, qkv_b)
-
-
-def attend_backward(qkv_b, kv_prompt, g_att, att, lse, prompt_rows):
-    tokens = qkv_b.shape[0]
-    prompt_len = kv_prompt.shape[0]
-    cont_len = tokens - prompt_rows
+    )(q, kp, vp, kc, vc)
+
+
+def attend_backward(q, kp, vp, kc, vc, g_att, att, lse, prompt_rows):
+    tokens, prompt_len, cont_len = q.shape[0], kp.shape[0], kc.shape[0]
     pairs = HEADS // 2
 
-    def kernel(q, kp, vp, ko, vo, g, a, ls, dq, dkp, dvp, dkc, dvc, accum):
+    def kernel(q, kp, vp, kc, vc, g, a, ls, dq, dkp, dvp, dkc, dvc, accum):
         attend_bwd_pair(
             lax.axis_index("shard"),
             prompt_rows,
             q,
             kp,
             vp,
-            ko.at[prompt_rows:, :],
-            vo.at[prompt_rows:, :],
+            kc,
+            vc,
             g,
             a,
             ls.at[0],
@@ -243,37 +229,18 @@
     def columns(rows):
         return pl.BlockSpec((rows, PAIR), lambda p: (0, p))
 
+    sizes = (tokens, prompt_len, prompt_len, cont_len, cont_len)
     return pl.pallas_call(
         kernel,
         grid=(pairs,),
-        in_specs=[
-            columns(tokens),
-            columns(prompt_len),
-            pl.BlockSpec((prompt_len, PAIR), lambda p: (0, pairs + p)),
-            pl.BlockSpec((tokens, PAIR), lambda p: (0, pairs + p)),
-            pl.BlockSpec((tokens, PAIR), lambda p: (0, 2 * pairs + p)),
-            columns(tokens),
-            columns(tokens),
-            pl.BlockSpec((1, 8, tokens), lambda p: (p, 0, 0)),
-        ],
-        out_specs=[
-            columns(tokens),
-            columns(prompt_len),
-            columns(prompt_len),
-            columns(cont_len),
-            columns(cont_len),
-        ],
-        out_shape=[
-            jax.ShapeDtypeStruct((tokens, D), jnp.bfloat16),
-            jax.ShapeDtypeStruct((prompt_len, D), jnp.bfloat16),
-            jax.ShapeDtypeStruct((prompt_len, D), jnp.bfloat16),
-            jax.ShapeDtypeStruct((cont_len, D), jnp.bfloat16),
-            jax.ShapeDtypeStruct((cont_len, D), jnp.bfloat16),
-        ],
+        in_specs=[columns(rows) for rows in sizes + (tokens, tokens)]
+        + [pl.BlockSpec((1, 8, tokens), lambda p: (p, 0, 0))],
+        out_specs=[columns(rows) for rows in sizes],
+        out_shape=[jax.ShapeDtypeStruct((rows, D), jnp.bfloat16) for rows in sizes],
         scratch_shapes=[pltpu.VMEM((PAIR, tokens), jnp.float32)],
         compiler_params=pltpu.CompilerParams(vmem_limit_bytes=VMEM_ALL),
         name="attend_backward",
-    )(qkv_b, kv_prompt, kv_prompt, qkv_b, qkv_b, g_att, att, lse)
+    )(q, kp, vp, kc, vc, g_att, att, lse)
 
 
 MESH_ID = pl.DeviceIdType.MESH
@@ -571,6 +538,321 @@
     return out.reshape(pieces, rows, width), out_s.reshape(4 * rows, s_width)
 
 
+def project_and_attend(prompt, conts, w_qkv, w_out, w_in, w_ffo, layer_biases):
+    pieces, early = 12, 6
+    rows = w_qkv.shape[0]
+    p_rows, cont_len = prompt.shape[0], conts.shape[0]
+    tokens = p_rows + cont_len
+    p_len = 4 * p_rows
+    pairs = HEADS // 2
+    tiles = tokens // TILE
+    chunk = 2 * PAIR
+    chunks = D // chunk
+    half_rows = rows // 2
+
+    def kernel(
+        xp, xc, wq, wo, wi, wf, bias, w_all_out, wf_out, q_out, kc_out, vc_out, kp_out, vp_out, att_out, lse,
+        stage, w_all, q, kc, vc, kp, vp, att,
+        load, c_s, c_r, x_s, x_r, y_s, y_r, d_s, d_r, e_s, e_r, w_sem,
+        kc_s, kc_r, kx_s, kx_r, kd_s, kd_r, out_sem,
+    ):
+        rep, shard = lax.axis_index("rep"), lax.axis_index("shard")
+        z, y = rep // 2, rep % 2
+        x, core = shard // 2, shard % 2
+        partner = (rep, 2 * x + 1 - core)
+        across = (rep, 2 * (1 - x) + core)
+        beside = (2 * z + 1 - y, shard)
+        there = 2 * (1 - x) + core
+
+        def remote(ref, send, recv, device):
+            return pltpu.make_async_remote_copy(
+                src_ref=ref,
+                dst_ref=ref,
+                send_sem=send,
+                recv_sem=recv,
+                device_id=device,
+                device_id_type=MESH_ID,
+            )
+
+        def source(k):
+            if k < 3:
+                j = (1, 2, 0)[k]
+                return wq.at[:, j * D : (j + 1) * D]
+            if k < 4:
+                return wo
+            if k < 8:
+                return wi.at[:, (k - 4) * D : (k - 3) * D]
+            return wf.at[(k - 8) * rows : (k - 7) * rows, :]
+
+        def loading(k):
+            return pltpu.make_async_copy(source(k), stage.at[k], load.at[k])
+
+        for k in range(pieces):
+            loading(k).start()
+        barrier = pltpu.get_barrier_semaphore()
+        for other in (partner, across, beside):
+            pl.semaphore_signal(barrier, inc=1, device_id=other, device_id_type=MESH_ID)
+        pl.semaphore_wait(barrier, 3)
+
+        def part(k, block, which):
+            return w_all.at[k, block, pl.ds(pl.multiple_of(which * half_rows, 16), half_rows), :]
+
+        def core_copy(k):
+            return remote(w_all.at[k, shard], c_s.at[k], c_r.at[k], partner)
+
+        def core_arrival(k):
+            return remote(w_all.at[k, 2 * x + 1 - core], c_s.at[k], c_r.at[k], partner)
+
+        def x_copy(k):
+            return remote(part(k, shard, y), x_s.at[k], x_r.at[k], across)
+
+        def x_arrival(k):
+            return remote(part(k, there, y), x_s.at[k], x_r.at[k], across)
+
+        def y_copy(k):
+            return remote(part(k, there, y), y_s.at[k], y_r.at[k], beside)
+
+        def y_arrival(k):
+            return remote(part(k, there, 1 - y), y_s.at[k], y_r.at[k], beside)
+
+        def d_copy(k):
+            return remote(part(k, there, y), d_s.at[k], d_r.at[k], partner)
+
+        def e_copy(k):
+            return remote(part(k, there, 1 - y), e_s.at[k], e_r.at[k], partner)
+
+        far = 2 * (1 - x) + 1 - core
+
+        def send_piece(k):
+            x_copy(k).start()
+            core_copy(k).start()
+
+        def round_piece(k):
+            loading(k).wait()
+            w_all[k, shard] = stage[k].astype(jnp.bfloat16)
+
+        def serve_x(k):
+            x_arrival(k).wait_recv()
+            y_copy(k).start()
+            d_copy(k).start()
+
+        def serve_y(k):
+            y_arrival(k).wait_recv()
+            e_copy(k).start()
+
+        def w_store(k):
+            if k < 8:
+                return pltpu.make_async_copy(w_all.at[k], w_all_out.at[k], w_sem.at[k])
+            return pltpu.make_async_copy(w_all.at[k], wf_out.at[:, k - 8], w_sem.at[k])
+
+        def complete(k):
+            core_arrival(k).wait_recv()
+            remote(part(k, far, y), d_s.at[k], d_r.at[k], partner).wait_recv()
+            remote(part(k, far, 1 - y), e_s.at[k], e_r.at[k], partner).wait_recv()
+            w_store(k).start()
+
+        def weight(k):
+            return w_all[k].reshape(4 * rows, D)
+
+        for k in range(early):
+            round_piece(k)
+            send_piece(k)
+        for k in range(early, pieces):
+            round_piece(k)
+        for k in range(3):
+            serve_x(k)
+        for k in range(3):
+            serve_y(k)
+
+        own_rows = pl.ds(pl.multiple_of(shard * p_rows, p_rows), p_rows)
+        kv = (kp, vp)
+
+        def kv_part(t, g, block):
+            lanes = pl.ds(g * chunk if isinstance(g, int) else pl.multiple_of(g * chunk, chunk), chunk)
+            return kv[t].at[pl.ds(pl.multiple_of(block * p_rows, p_rows), p_rows), lanes]
+
+        def kv_core(t, g):
+            return remote(kv_part(t, g, shard), kc_s.at[g, t], kc_r.at[g, t], partner)
+
+        def kv_across(t, g):
+            return remote(kv_part(t, g, shard), kx_s.at[g, t], kx_r.at[g, t], across)
+
+        def kv_forward(t, g):
+            return remote(kv_part(t, g, there), kd_s.at[g, t], kd_r.at[g, t], partner)
+
+        complete(0)
+        kp[own_rows, :] = dot_plain(xp[...], weight(0)).astype(jnp.bfloat16)
+        complete(1)
+        vp[own_rows, :] = (dot_plain(xp[...], weight(1)) + bias[1:2, :]).astype(jnp.bfloat16)
+        for g in range(chunks):
+            for t in range(2):
+                kv_across(t, g).start()
+                kv_core(t, g).start()
+        for k in range(early, pieces):
+            send_piece(k)
+        kc[...] = dot_plain(xc[...], weight(0)).astype(jnp.bfloat16)
+        vc[...] = (dot_plain(xc[...], weight(1)) + bias[1:2, :]).astype(jnp.bfloat16)
+        complete(2)
+        q[:p_rows, :] = (dot_plain(xp[...], weight(2)) + bias[0:1, :]).astype(jnp.bfloat16)
+        q[p_rows:, :] = (dot_plain(xc[...], weight(2)) + bias[0:1, :]).astype(jnp.bfloat16)
+
+        def keep(ref, target, i):
+            return pltpu.make_async_copy(ref, target, out_sem.at[i])
+
+        kept = [(q, q_out, 0), (kc, kc_out, 1), (vc, vc_out, 2)]
+        for item in kept:
+            keep(*item).start()
+
+        def serve_kv(g):
+            for t in range(2):
+                remote(kv_part(t, g, there), kx_s.at[g, t], kx_r.at[g, t], across).wait_recv()
+                kv_forward(t, g).start()
+
+        def complete_kv(g):
+            for t in range(2):
+                remote(
+                    kv_part(t, g, 2 * x + 1 - core), kc_s.at[g, t], kc_r.at[g, t], partner
+                ).wait_recv()
+                remote(kv_part(t, g, far), kd_s.at[g, t], kd_r.at[g, t], partner).wait_recv()
+
+        serve_kv(0)
+        first_slot = {3: 0, 4: 1, 5: 2}
+        for k in range(early, pieces):
+            first_slot[k] = 10 + 2 * (k - early)
+        slots = pairs * tiles
+        work = []
+        for k in range(3, pieces):
+            work += [(first_slot[k], serve_x, k), (first_slot[k] + 2, serve_y, k)]
+            work.append((first_slot[k] + 4, complete, k))
+        work.sort(key=lambda item: item[0])
+
+        def att_store(p):
+            lanes = pl.ds(pl.multiple_of(p * PAIR, PAIR), PAIR)
+            return pltpu.make_async_copy(att.at[:, lanes], att_out.at[:, lanes], out_sem.at[5 + p])
+
+        def pair(p, carry):
+            @pl.when(p % 2 == 0)
+            def _():
+                complete_kv(p // 2)
+
+            def between(tile):
+                @pl.when((p % 2 == 0) & (p < pairs - 2) & (tile == tiles - 1))
+                def _():
+                    serve_kv(p // 2 + 1)
+
+                for slot, action, k in work:
+                    if slot < slots and slot % tiles == tile:
+
+                        @pl.when(p == slot // tiles)
+                        def _(action=action, k=k):
+                            action(k)
+
+            lanes = pl.ds(pl.multiple_of(p * PAIR, PAIR), PAIR)
+            attend_fwd_pair(
+                shard,
+                p_rows,
+                q.at[:, lanes],
+                kp.at[:, lanes],
+                vp.at[:, lanes],
+                kc.at[:, lanes],
+                vc.at[:, lanes],
+                att.at[:, lanes],
+                lse.at[p],
+                between,
+            )
+            att_store(p).start()
+            return carry
+
+        lax.fori_loop(0, pairs, pair, 0)
+        kept += [(kp, kp_out, 3), (vp, vp_out, 4)]
+        for item in kept[3:]:
+            keep(*item).start()
+        for slot, action, k in work:
+            if slot >= slots:
+                action(k)
+        for item in kept:
+            keep(*item).wait()
+
+        def last_pair(p, carry):
+            att_store(p).wait()
+            return carry
+
+        lax.fori_loop(0, pairs, last_pair, 0)
+        for k in range(pieces):
+            w_store(k).wait()
+            for copy in (core_copy, x_copy, y_copy, d_copy, e_copy):
+                copy(k).wait_send()
+        for g in range(chunks):
+            for t in range(2):
+                for copy in (kv_core, kv_across, kv_forward):
+                    copy(t, g).wait_send()
+
+    def sems(*dims):
+        return pltpu.SemaphoreType.DMA(dims)
+
+    def low(*dims):
+        return jax.ShapeDtypeStruct(dims, jnp.bfloat16)
+
+    anywhere = pl.BlockSpec(memory_space=pl.ANY)
+    vmem = pl.BlockSpec(memory_space=pltpu.VMEM)
+    n = pieces
+    out = pl.pallas_call(
+        kernel,
+        in_specs=[vmem, vmem, anywhere, anywhere, anywhere, anywhere, vmem],
+        out_specs=[anywhere] * 8 + [vmem],
+        out_shape=[
+            low(8, 4, rows, D),
+            low(4, 4, rows, D),
+            low(tokens, D),
+            low(cont_len, D),
+            low(cont_len, D),
+            low(p_len, D),
+            low(p_len, D),
+            jax.ShapeDtypeStruct((tokens, D), jnp.float32),
+            jax.ShapeDtypeStruct((pairs, 8, tokens), jnp.float32),
+        ],
+        scratch_shapes=[
+            pltpu.VMEM((n, rows, D), jnp.float32),
+            pltpu.VMEM((n, 4, rows, D), jnp.bfloat16),
+            pltpu.VMEM((tokens, D), jnp.bfloat16),
+            pltpu.VMEM((cont_len, D), jnp.bfloat16),
+            pltpu.VMEM((cont_len, D), jnp.bfloat16),
+            pltpu.VMEM((p_len, D), jnp.bfloat16),
+            pltpu.VMEM((p_len, D), jnp.bfloat16),
+            pltpu.VMEM((tokens, D), jnp.float32),
+        ]
+        + [sems(n)] * 12
+        + [sems(chunks, 2)] * 6
+        + [sems(5 + pairs)],
+        compiler_params=pltpu.CompilerParams(
+            collective_id=1, has_side_effects=True, vmem_limit_bytes=VMEM_ALL
+        ),
+        name="project_and_attend",
+    )(prompt, conts, w_qkv, w_out, w_in, w_ffo, layer_biases)
+    w_all, wf, q, kc, vc, kp, vp, att, lse = out
+    w_all = w_all.reshape(8, 4 * rows, D)
+    return w_all, wf.reshape(16 * rows, D), q, kp, vp, kc, vc, att, lse
+
+
+def project_native(prompt, conts, w_qkv, w_out, w_in, w_ffo, layer_biases):
+    rows = prompt.shape[0]
+
+    def gathered(value):
+        return lax.all_gather(value.astype(jnp.bfloat16), "shard", axis=0, tiled=True)
+
+    qkv, out, inner, ffo = (gathered(w) for w in (w_qkv, w_out, w_in, w_ffo))
+    tokens = jnp.concatenate([prompt, conts], 0)
+    bias = jnp.concatenate([layer_biases[0], jnp.zeros((D,), jnp.float32), layer_biases[1]])
+    qkv_b = (dot_plain(tokens, qkv) + bias).astype(jnp.bfloat16)
+    q, keys, values = (qkv_b[:, i * D : (i + 1) * D] for i in range(3))
+    kp, vp = gathered(keys[:rows]), gathered(values[:rows])
+    kc, vc = keys[rows:], values[rows:]
+    att, lse = attend_forward(q, kp, vp, kc, vc, rows)
+    blocks = [qkv[:, D : 2 * D], qkv[:, 2 * D :], qkv[:, :D], out]
+    blocks += [inner[:, i * D : (i + 1) * D] for i in range(inner.shape[1] // D)]
+    return jnp.stack(blocks), ffo, q, kp, vp, kc, vc, att, lse
+
+
 def student_loss(stu_rows, pool_query, bias_pool, w_pool, w_class, bias_class, label_value):
     part_w = STU // SHEADS
     parts = stu_rows.reshape(stu_rows.shape[0], SHEADS, part_w)
@@ -661,23 +943,15 @@
     prompt_rows = prompt.shape[1]
     cont_len = conts.shape[2]
     prompt_len = prompt_rows * lax.axis_size("shard")
-    qkv_low = w_qkv.astype(jnp.bfloat16)
-    out_low = w_out.astype(jnp.bfloat16)
-    in_low = w_in.astype(jnp.bfloat16)
-    ffo_low = w_ffo.astype(jnp.bfloat16)
-    qkv_full, out_full, in_full, ffo_full = (
-        lax.all_gather(qkv_low, "shard", axis=0, tiled=True),
-        lax.all_gather(out_low, "shard", axis=0, tiled=True),
-        lax.all_gather(in_low, "shard", axis=0, tiled=True),
-        lax.all_gather(ffo_low, "shard", axis=0, tiled=True),
-    )
+    direct = (lax.axis_size("rep"), lax.axis_size("shard")) == (8, 4)
+    project = project_and_attend if direct else project_native
+    w_all, ffo_full, q, kp, vp, kc, vc, attended, log_totals = project(
+        prompt[0], conts[0, 0], w_qkv, w_out, w_in, w_ffo, layer_biases
+    )
+    out_full = w_all[3]
+    in_full = jnp.concatenate([w_all[4], w_all[5], w_all[6], w_all[7]], 1)
     tokens = jnp.concatenate([prompt[0], conts[0, 0]], 0)
     tokens_f = tokens.astype(jnp.float32)
-    zero_row = jnp.zeros((D,), jnp.float32)
-    bias_three = jnp.concatenate([layer_biases[0], zero_row, layer_biases[1]])
-    qkv_b = (dot_plain(tokens, qkv_full) + bias_three).astype(jnp.bfloat16)
-    kv_prompt = lax.all_gather(qkv_b[:prompt_rows, D:], "shard", axis=0, tiled=True)
-    attended, log_totals = attend_forward(qkv_b, kv_prompt, prompt_rows)
     att_b = attended.astype(jnp.bfloat16)
     branch = dot_plain(att_b, out_full) + layer_biases[2]
     resid_one = tokens_f + branch
@@ -717,12 +991,7 @@
     g_output = g_output + jnp.concatenate(
         [jnp.zeros((prompt_rows, D), jnp.float32), student_back], 0
     )
-    qkv_back, out_back, in_back, ffo_back = (
-        lax.all_gather(qkv_low, "shard", axis=0, tiled=True),
-        lax.all_gather(out_low, "shard", axis=0, tiled=True),
-        lax.all_gather(in_low, "shard", axis=0, tiled=True),
-        lax.all_gather(ffo_low, "shard", axis=0, tiled=True),
-    )
+    out_back, in_back, ffo_back = out_full, in_full, ffo_full
     norm_two, norm_two_pull = jax.vjp(layer_norm, resid_two, norm_gains[1], layer_biases[5])
     g_resid_two, g_gain_two, g_shift_two = norm_two_pull(g_output)
     g_ffn_b = g_resid_two.astype(jnp.bfloat16)
@@ -741,14 +1010,14 @@
     g_out_bias = jnp.sum(g_branch_b.astype(jnp.float32), 0)
     g_att_b = dot_second(g_branch_b, out_back).astype(jnp.bfloat16)
     query_grad_b, g_keys_p, g_values_p, g_keys_c, g_values_c = attend_backward(
-        qkv_b, kv_prompt, g_att_b, attended, log_totals, prompt_rows
+        q, kp, vp, kc, vc, g_att_b, attended, log_totals, prompt_rows
     )
     cont_kv_b = jnp.concatenate([g_keys_c, g_values_c], 1)
     block_kv_b = jnp.concatenate([g_keys_p, g_values_p], 1)
-    kv_weights = qkv_back[:, D:]
+    kv_weights = jnp.concatenate([w_all[0], w_all[1]], 1)
     g_query_w = dot_first(tokens, query_grad_b)
     g_kv_w = dot_first(tokens[prompt_rows:], cont_kv_b)
-    g_tokens = g_resid_one + dot_second(query_grad_b, qkv_back[:, :D])
+    g_tokens = g_resid_one + dot_second(query_grad_b, w_all[2])
     cont_through = dot_second(cont_kv_b, kv_weights)
     kv_summed = lax.psum_scatter(
         block_kv_b,
@@ -780,7 +1049,6 @@
     g_gains = jnp.stack([g_gain_one, g_gain_two])
     g_vectors = jnp.stack([g_sbias, g_query, g_pbias])
     small = (g_biases, g_gains, g_in_bias, g_student, g_vectors, g_pool, g_class, g_cbias)
-    direct = (lax.axis_size("rep"), lax.axis_size("shard")) == (8, 4)
     owned, summed = (sum_direct if direct else sum_native)(g_qkvw, g_outw, g_in, g_ffo, small)
     owned_qkv, owned_out, owned_in, owned_ffo = owned
     return (

time: 477 us -> 431 us (0.904)
  waiting for transfers between devices: 99.3 us -> 10.9 us
  Pallas kernels: 177 us -> 238 us
  matrix products: 102 us -> 92.3 us
  other arithmetic: 35.5 us -> 30.4 us
    all_gather x5 -> x0, waiting for transfers between devices: 95.3 us -> none  [the longest x1 33.2 us: body(): lax.all_gather(qkv_low, 'shard', axis=0, tiled=True)]
    pallas_call x2, Pallas kernels: 62.6 us -> 123 us  [the longest x1 85.2 us: project_and_attend(): pl.pallas_call(kernel, in_specs=[vmem, vmem, anywhere, anywhere, anywhere...]
    unnamed x142 -> x132, local copies, waits for them, and re-layouts: 17.7 us -> 8.57 us
    dot_general x5 -> x4, matrix products: 47.2 us -> 39.1 us  [dot_plain(): return jnp.dot(left, right, preferred_element_type=jnp.float32)]
    convert_element_type x4 -> x0, other arithmetic: 7.36 us -> none  [the longest x1 2.88 us: body(): ffo_low = w_ffo.astype(jnp.bfloat16)]
    reduce_scatter x1, waiting for transfers between devices: 3.85 us -> 10.8 us  [body(): lax.psum_scatter(block_kv_b, 'shard', scatter_dimension=0, tiled=True)]
    slice x1, local copies, waits for them, and re-layouts: 0.93 us -> 5.92 us  [body(): g_tokens = g_resid_one + dot_second(query_grad_b, w_all[2])]
  transfers between devices with their start and end apart: 6 -> 1, of which waited for: 5 -> 1; matrix products, arithmetic and copies ran while one was open for 15% -> 7% of each run, Pallas kernels for 5% -> 0%
where the time goes in v2:
time: 431 us; the launch traced here: 423 us
  Pallas kernels  238 us (55%)
  matrix products  92.3 us (21%)
  local copies, waits for them, and re-layouts  33.5 us (8%)
  other arithmetic  30.4 us (7%)
  between operations  18.1 us (4%)
  waiting for transfers between devices  10.9 us (3%)
    pallas_call x1, Pallas kernels, sum_gradients(): pl.pallas_call(kernel, in_specs=[anywhere] * 5, out_specs=[anywhere, pl.B...  115 us
    pallas_call x1, Pallas kernels, project_and_attend(): pl.pallas_call(kernel, in_specs=[vmem, vmem, anywhere, anywhere, anywhere...  85.2 us
    dot_general x4, matrix products, dot_plain(): return jnp.dot(left, right, preferred_element_type=jnp.float32)  39.1 us
    pallas_call x1, Pallas kernels, attend_backward(): pl.pallas_call(kernel, grid=(pairs,), in_specs=[columns(rows) for rows in...  37.8 us
    dot_general x6, matrix products, dot_second(): lax.dot_general(left, right, (((1,), (1,)), ((), ())), preferred_element_...  26.7 us
    dot_general x6, matrix products, dot_first(): lax.dot_general(left, right, (((0,), (0,)), ((), ())), preferred_element_...  20.4 us
    reduce_scatter x1, waiting for transfers between devices, body(): lax.psum_scatter(block_kv_b, 'shard', scatter_dimension=0, tiled=True)  10.8 us
  transfers between devices with their start and end apart: 1, of which 1 were waited for; matrix products, arithmetic and copies ran while one was open for 7% of the time, Pallas kernels for 0%

profile of v2, /device:TPU:0, one launch (start us, length us, event | category | flops | bytes accessed | tf_op | source)
XLA Modules:
  0.0 422.9 jit_solution(1613464838647398124)
XLA Ops:
  7.3 85.2 %project_and_attend.1 = (bf16[8,4,192,768]{3,2,1,0:T(8,128)(2,1)}, bf16[4,4,192,768]{3,2,1,0:T(8,128)(2,1)}, bf16[768,768]{1,0:T(8,128)(2,1)}, bf16[512,768]{1,0...) custom-call(bf16[256,768]{1,0:T(8,128)(2,1)} %bitcast.177, ...), custom_call_target="tpu_custom_call" | custom-call | tf_op jit(solution)/shard_map/project_and_attend/pallas_call | solution.py:799
  92.5 5.9 %fusion.63 = (bf16[1,4,192,768]{3,2,1,0:T(8,128)(2,1)}, bf16[1,4,192,768]{3,2,1,0:T(8,128)(2,1)}, bf16[1,4,192,768]{3,2,1,0:T(8,128)(2,1)}, bf16[1,4,192,768]{3,...) fusion(bf16[8,4,192,768]{3,2,1,0:T(8,128)(2,1)} %get-tuple-elem, ...), kind=kLoop, calls=%fused_computation.156 | loop fusion | bytes 18874368 | tf_op jit(solution)/shard_map/slice | solution.py:1020
  101.0 30.1 %multiply_convert_fusion = (bf16[768,3072]{1,0:T(8,128)(2,1)}, f32[768,3072]{1,0:T(8,128)}, f32[768,3072]{1,0:T(8,128)}) fusion(f32[3072]{0:T(1024)S(1)} %copy-done.57, bf16[768,768]{1,0:T(8,128)(2,1)S(1)} %bitcast.188, bf16[768,768]{1,0:T(8,128)(2,1)S(1)} %bitcast.190, bf16[768,768]{1,0:T(8,128)(2,1)S(1)} %bitcast.192, bf16[768,768]{1,0:T(8,128)(2,1)S(1)} %bitcast.194, ...), kind=kOutput, calls=%fused_computation.3 | convolution fusion | flops 3801415680 | bytes 30695424 | tf_op jit(solution)/shard_map/dot_general | solution.py:20
  131.1 7.4 %fusion.66 = (f32[768]{0:T(1024)S(1)}, f32[768,768]{1,0:T(8,128)S(1)}) fusion(f32[768]{0:T(1024)S(1)} %get-tuple-element.58, bf16[768,3072]{1,0:T(8,128)(2,1)} %get-tuple-element.81, bf16[3072,768]{1,0:T(8,128)(2,1)} %bitcast.207, f32[768]{0:T(1024)S(1)} %get-tuple-element.56, f32[768]{0:T(1024)S(1)} %get-tuple-element.112, f32[768]{0:T(1024)S(1)} %fusion.31, ...), kind=kOutput, calls=%fused_computation.159 | convolution fusion | flops 3628006656 | bytes 14174208 | tf_op jit(solution)/shard_map/dot_general | solution.py:20
  144.0 1.4 fusion.67
  147.4 1.3 fusion.33
  155.9 1.4 fusion.20
  157.3 1.8 multiply_reduce_fusion
  159.2 1.8 fusion.58
  161.8 12.6 %fusion.54 = (bf16[3072]{0:T(1024)(128)(2,1)S(1)}, bf16[768,3072]{1,0:T(8,128)(2,1)}) fusion(f32[768,3072]{1,0:T(8,128)} %get-tuple-element.82, f32[768,3072]{1,0:T(8,128)} %get-tuple-element.106, f32[3072]{0:T(1024)S(1)} %copy-done.58, bf16[768,768]{1,0:T(8,128)(2,1)S(1)} %get-tuple-element.68, bf16[3072,768]{1,0:T(8,128)(2,1)S(1)} %bitcast.210), kind=kOutput, calls=%fused_computation.149 | convolution fusion | flops 3661624320 | bytes 29509632 | tf_op jit(solution)/shard_map/dot_general | solution.py:30
  174.5 6.8 %multiply_reduce_fusion.1 = (bf16[768]{0:T(1024)(128)(2,1)S(1)}, f32[768]{0:T(1024)S(1)}, bf16[768]{0:T(1024)(128)(2,1)S(1)}, f32[768,768]{1,0:T(8,128)S(1)}) fusion(f32[768,768]{1,0:T(8,128)S(1)} %copy-done.4, f32[768]{0:T(1024)S(1)} %fusion.31, f32[768]{0:T(1024)S(1)} %broadcast_multiply_fusion.1, f32[768]{0:T(1024)S(1)} %get-tuple-element.112, ...), kind=kOutput, calls=%fused_computation.30 | convolution fusion | flops 3648648960 | bytes 16533504 | tf_op jit(solution)/shard_map/dot_general | solution.py:30
  183.7 2.1 convolution_convert_fusion.4.g
  185.8 37.8 %attend_backward.1 = (bf16[768,768]{1,0:T(8,128)(2,1)}, bf16[1024,768]{1,0:T(8,128)(2,1)}, bf16[1024,768]{1,0:T(8,128)(2,1)}, bf16[512,768]{1,0:T(8,128)(2,1)}, bf16[512,768]{1,0:T(8,128)(2,1)}) custom-call(bf16[768,768]{1,0:T(8,128)(2,1)} %get-tuple-element.36.q, bf16[1024,768]{1,0:T(8,128)(2,1)} %get-tuple-element.37.kp, ...), custom_call_target="tpu_custom_call" | custom-call | tf_op jit(solution)/shard_map/attend_backward/pallas_call | solution.py:233
  223.6 3.7 pad_maximum_fusion.2
  228.8 1.5 reduce.1
  230.5 1.3 constant_dynamic-update-slice_fusion.1
  236.1 2.1 convolution_convert_fusion.3
  239.0 2.2 convolution_convert_fusion.2.go
  241.3 2.6 fusion.8
  243.9 5.6 %convolution_convert_fusion.gf = bf16[3072,768]{1,0:T(8,128)(2,1)} fusion(bf16[768,3072]{1,0:T(8,128)(2,1)S(1)} %bitcast.214, bf16[768,768]{1,0:T(8,128)(2,1)S(1)} %copy-done.44), kind=kOutput, calls=%fused_computation.17 | convolution fusion | flops 3626237952 | bytes 10616832 | tf_op jit(solution)/shard_map/dot_general | solution.py:24
  249.5 6.5 %convolution_convert_fusion.1.gi = bf16[768,3072]{1,0:T(8,128)(2,1)} fusion(bf16[768,3072]{1,0:T(8,128)(2,1)S(1)} %bitcast.212, f32[768,768]{1,0:T(8,128)S(1)} %copy-done.5, f32[768]{0:T(1024)S(1)} %get-tuple-element.56, f32[768]{0:T(1024)S(1)} %get-tuple-element.112, f32[768]{0:T(1024)S(1)} %fusion.31, f32[768]{0:T(1024)S(1)} %broadcast_multiply_fusion.1), kind=kOutput, calls=%fused_computation.18 | convolution fusion | flops 3629187072 | bytes 11808768 | tf_op jit(solution)/shard_map/dot_general | solution.py:24
  256.0 10.8 %reduce-scatter.2.cloned.1.call-done = bf16[256,1536]{1,0:T(8,128)(2,1)} async-done(((bf16[1024,1536]{1,0:T(8,128)(2,1)}), bf16[256,1536]{1,0:T(8,128)(2,1)}) %reduce-scatter.2.cloned.1.call-update) | async-done | bytes 786448 | tf_op jit(solution)/shard_map/reduce_scatter | solution.py:1022
  268.0 2.2 fusion.46
  270.2 2.8 fusion.6
  273.1 1.5 concatenate.51
  274.6 1.7 pad_maximum_fusion.12.gs
  276.3 4.0 pad_maximum_fusion.1.gq
  280.3 114.7 %sum_gradients.1 = (bf16[12,4,48,768]{3,2,1,0:T(8,128)(2,1)}, bf16[4,4,48,256]{3,2,1,0:T(8,128)(2,1)}) custom-call(bf16[768,2304]{1,0:T(8,128)(2,1)} %pad_maximum_fusion.1.gq, bf16[768,768]{1,0:T(8,128)(2,1)} %convolution_convert_fusion.2.go, bf16[768,3072]{1,0:T(8,128)(2,1)} %convolution_convert_fusion.1.gi, bf16[3072,768]{1,0:T(8,128)(2,1)} %convolution_convert_fusion.gf, ...), custom_call_target="tpu_custom_call" | custom-call | tf_op jit(solution)/shard_map/sum_gradients/pallas_call | solution.py:518
  395.0 3.9 fusion.64
  399.0 1.7 slice.198
  411.3 2.6 pad_maximum_fusion.5
  413.9 1.7 pad_maximum_fusion.4
  (224 shorter events, 36.0 us)
Async XLA Ops:
  7.2 136.6 %copy-start = (f32[128,128]{1,0:T(8,128)S(1)}, f32[128,128]{1,0:T(8,128)}, u32[]{:S(2)}) copy-start(f32[128,128]{1,0:T(8,128)} %param.31) | copy-start | bytes 196612
  7.2 259.7 %reduce-scatter.2.cloned.1.call-start = ((), (), s32[]{:S(2)}) async-start(), calls=%async_computation.1 | async-start | bytes 3932160 | tf_op jit(solution)/shard_map/reduce_scatter | solution.py:1022
  92.4 6.0 %copy-start.50 = (f32[6,768]{1,0:T(8,128)S(1)}, f32[6,768]{1,0:T(8,128)}, u32[]{:S(2)}) copy-start(f32[6,768]{1,0:T(8,128)} %bias.1) | copy-start | bytes 55300
  92.4 6.0 %copy-start.52 = (f32[2,768]{1,0:T(2,128)S(1)}, f32[2,768]{1,0:T(2,128)}, u32[]{:S(2)}) copy-start(f32[2,768]{1,0:T(2,128)} %param.27) | copy-start | bytes 18436
  92.4 6.1 %copy-start.14 = (bf16[1,1,512,768]{3,2,1,0:T(8,128)(2,1)S(1)}, bf16[1,1,512,768]{3,2,1,0:T(8,128)(2,1)}, u32[]{:S(2)}) copy-start(bf16[1,1,512,768]{3,2,1,0:T(8,128)(2,1)} %param.18) | copy-start | bytes 2359300
  92.5 6.1 %copy-start.22 = (f32[768,768]{1,0:T(8,128)S(1)}, f32[768,768]{1,0:T(8,128)}, u32[]{:S(2)}) copy-start(f32[768,768]{1,0:T(8,128)} %get-tuple-element.33.a) | copy-start | bytes 7077892
  92.5 6.1 %copy-start.24 = (bf16[1,256,768]{2,1,0:T(8,128)(2,1)S(1)}, bf16[1,256,768]{2,1,0:T(8,128)(2,1)}, u32[]{:S(2)}) copy-start(bf16[1,256,768]{2,1,0:T(8,128)(2,1)} %param.17) | copy-start | bytes 1179652
  99.8 31.3 %copy-start.3 = (f32[768,768]{1,0:T(8,128)}, f32[768,768]{1,0:T(8,128)S(1)}, u32[]{:S(2)}) copy-start(f32[768,768]{1,0:T(8,128)S(1)} %get-tuple-element.105) | copy-start | bytes 7077892
  139.8 4.2 copy-start.51
  145.4 13.7 %copy-start.53 = (f32[14]{0:T(128)}, f32[14]{0:T(128)S(1)}, u32[]{:S(2)}) copy-start(f32[14]{0:T(128)S(1)} %get-tuple-element.110) | copy-start | bytes 172
  161.3 13.2 %copy-start.43 = (bf16[768,768]{1,0:T(8,128)(2,1)}, bf16[768,768]{1,0:T(8,128)(2,1)S(1)}, u32[]{:S(2)}) copy-start(bf16[768,768]{1,0:T(8,128)(2,1)S(1)} %get-tuple-element.68) | copy-start | bytes 3538948
  161.8 12.7 %copy-start.4 = (f32[768,768]{1,0:T(8,128)S(1)}, f32[768,768]{1,0:T(8,128)}, u32[]{:S(2)}) copy-start(f32[768,768]{1,0:T(8,128)} %copy-done.3) | copy-start | bytes 7077892
  161.8 12.7 %copy-start.36 = (bf16[1,4,192,768]{3,2,1,0:T(8,128)(2,1)S(1)}, bf16[1,4,192,768]{3,2,1,0:T(8,128)(2,1)}, u32[]{:S(2)}) copy-start(bf16[1,4,192,768]{3,2,1,0:T(8,128)(2,1)} %copy-done.35) | copy-start | bytes 3538948
  161.8 12.7 %copy-start.38 = (bf16[1,4,192,768]{3,2,1,0:T(8,128)(2,1)S(1)}, bf16[1,4,192,768]{3,2,1,0:T(8,128)(2,1)}, u32[]{:S(2)}) copy-start(bf16[1,4,192,768]{3,2,1,0:T(8,128)(2,1)} %copy-done.37) | copy-start | bytes 3538948
  161.8 12.7 %copy-start.40 = (bf16[1,4,192,768]{3,2,1,0:T(8,128)(2,1)S(1)}, bf16[1,4,192,768]{3,2,1,0:T(8,128)(2,1)}, u32[]{:S(2)}) copy-start(bf16[1,4,192,768]{3,2,1,0:T(8,128)(2,1)} %copy-done.39) | copy-start | bytes 3538948
  161.8 12.7 %copy-start.42 = (bf16[1,4,192,768]{3,2,1,0:T(8,128)(2,1)S(1)}, bf16[1,4,192,768]{3,2,1,0:T(8,128)(2,1)}, u32[]{:S(2)}) copy-start(bf16[1,4,192,768]{3,2,1,0:T(8,128)(2,1)} %copy-done.41) | copy-start | bytes 3538948
  230.4 3.6 copy-start.48
  233.0 8.3 %copy-start.6 = (bf16[512,1536]{1,0:T(8,128)(2,1)}, bf16[512,1536]{1,0:T(8,128)(2,1)S(1)}, u32[]{:S(2)}) copy-start(bf16[512,1536]{1,0:T(8,128)(2,1)S(1)} %constant_dynamic-update-slice_fusion) | copy-start | bytes 4718596
  236.1 7.8 %slice-start.4 = ((s8[4718592]{0:T(1024)(128)(4,1)}), s8[4194304]{0:T(1024)(128)(4,1)S(1)}, s32[]{:S(2)}) async-start(s8[4718592]{0:T(1024)(128)(4,1)} %bitcast.213), calls=%async_computation.6 | async-start | bytes 8388608
  239.0 4.8 %slice-start.5 = ((s8[4718592]{0:T(1024)(128)(4,1)}), s8[524288]{0:T(1024)(128)(4,1)S(1)}, s32[]{:S(2)}) async-start(s8[4718592]{0:T(1024)(128)(4,1)} %bitcast.213), calls=%async_computation.7 | async-start | bytes 1048576
  241.3 8.2 %slice-start.2 = ((s8[4718592]{0:T(1024)(128)(4,1)}), s8[4194304]{0:T(1024)(128)(4,1)S(1)}, s32[]{:S(2)}) async-start(s8[4718592]{0:T(1024)(128)(4,1)} %bitcast.211), calls=%async_computation.4 | async-start | bytes 8388608
  243.9 5.6 %copy-start.5 = (f32[768,768]{1,0:T(8,128)S(1)}, f32[768,768]{1,0:T(8,128)}, u32[]{:S(2)}) copy-start(f32[768,768]{1,0:T(8,128)} %copy-done.3) | copy-start | bytes 7077892
  243.9 5.6 %slice-start.3 = ((s8[4718592]{0:T(1024)(128)(4,1)}), s8[524288]{0:T(1024)(128)(4,1)S(1)}, s32[]{:S(2)}) async-start(s8[4718592]{0:T(1024)(128)(4,1)} %bitcast.211), calls=%async_computation.5 | async-start | bytes 1048576
  395.0 4.0 copy-start.2
  399.0 4.9 %copy-start.13 = (bf16[256,1536]{1,0:T(8,128)(2,1)S(1)}, bf16[256,1536]{1,0:T(8,128)(2,1)}, u32[]{:S(2)}) copy-start(bf16[256,1536]{1,0:T(8,128)(2,1)} %reduce-scatter.2.cloned.1.call-done) | copy-start | bytes 2359300
  399.0 4.9 %copy-start.30 = (bf16[1,4,192,768]{3,2,1,0:T(8,128)(2,1)S(1)}, bf16[1,4,192,768]{3,2,1,0:T(8,128)(2,1)}, u32[]{:S(2)}) copy-start(bf16[1,4,192,768]{3,2,1,0:T(8,128)(2,1)} %get-tuple-element.84) | copy-start | bytes 3538948
  399.0 4.9 %copy-start.32 = (bf16[1,4,192,768]{3,2,1,0:T(8,128)(2,1)S(1)}, bf16[1,4,192,768]{3,2,1,0:T(8,128)(2,1)}, u32[]{:S(2)}) copy-start(bf16[1,4,192,768]{3,2,1,0:T(8,128)(2,1)} %get-tuple-element.85) | copy-start | bytes 3538948
  407.2 4.1 copy-start.21
  408.5 5.4 %copy-start.17 = (f32[1,4,48,768]{3,2,1,0:T(8,128)S(1)}, f32[1,4,48,768]{3,2,1,0:T(8,128)}, u32[]{:S(2)}) copy-start(f32[1,4,48,768]{3,2,1,0:T(8,128)} %get-tuple-element.91) | copy-start | bytes 1769476
  408.5 5.4 %copy-start.18 = (f32[1,4,48,768]{3,2,1,0:T(8,128)S(1)}, f32[1,4,48,768]{3,2,1,0:T(8,128)}, u32[]{:S(2)}) copy-start(f32[1,4,48,768]{3,2,1,0:T(8,128)} %get-tuple-element.92) | copy-start | bytes 1769476
  408.5 5.4 %copy-start.19 = (f32[1,4,48,768]{3,2,1,0:T(8,128)S(1)}, f32[1,4,48,768]{3,2,1,0:T(8,128)}, u32[]{:S(2)}) copy-start(f32[1,4,48,768]{3,2,1,0:T(8,128)} %get-tuple-element.93) | copy-start | bytes 1769476
  408.5 5.4 %copy-start.20 = (f32[1,4,48,768]{3,2,1,0:T(8,128)S(1)}, f32[1,4,48,768]{3,2,1,0:T(8,128)}, u32[]{:S(2)}) copy-start(f32[1,4,48,768]{3,2,1,0:T(8,128)} %get-tuple-element.94) | copy-start | bytes 1769476
  (34 other events, 71.2 us)
Sparse Core Ops, SparseCore 0:
  227.5 39.2 reduce-scatter.1
